TPU v7x, 32 devices: a whole 2x2x4 slice. The times are simulated.
32 devices in a mesh: rep: 4 (over z), tp: 2 (over x), seq: 4 (over y, core).
Axes of the slice: x: 2, y: 2, z: 4, core: 2. Of those that a mesh axis runs over, the one named last changes fastest.
Arguments:
- prompt_x: bfloat16 [4, 4096, 8192], P('rep', 'seq'), may hold values from -6 to 6
- norm_gain: float32 [8192], replicated, may hold values from 0.1 to 1.9
- key_weight: bfloat16 [8192, 1024], P(None, 'tp'), may hold values from -0.0625 to 0.0625
- value_weight: bfloat16 [8192, 1024], P(None, 'tp'), may hold values from -0.0625 to 0.0625
- prompt_lengths: int32 [4], replicated, may hold values from 1024 to 4096
- page_table: int32 [4, 32], replicated, may hold values from 0 to 127, as said below
- request_slots: int32 [128], replicated, may hold values from 0 to 3
- queries: bfloat16 [4, 128, 8192], P(None, None, 'tp'), may hold values from -240 to 240
- new_kv: bfloat16 [2, 4, 128, 1024], P(None, None, ('rep', 'seq')), may hold values from -6 to 6
Outputs:
- attention: bfloat16 [4, 128, 8192], P(None, ('rep', 'seq'), 'tp')
- paged_cache: bfloat16 [128, 2, 128, 1024], P(('rep', 'seq'), None, None, 'tp')
Inputs may be any that keep to these rules, and one draw needn't show every extreme that they name: `page_table`: every page 0 to 127 is named once; page // 8 is the decode shard (index of rep times 4 plus index of seq) that holds it; the blocks b * 8 to b * 8 + 7 of one prompt go to 8 different shards. `request_slots`: several requests may continue one prompt. `prompt_lengths`: tokens at or past a prompt's length are padding.
All inputs are finite; a program needn't handle non-finite values.
Results may differ from a plain program's by a relative error of at most 0.02.
The roundings to bfloat16 on the way count: a program that leaves them out, or rounds other values in their place, can miss the bound.
Values may be sent and summed in bfloat16 or wider, within the bound.
A program may use at most 192 MiB of HBM per device.

v0:
```python
import functools

import jax
import jax.numpy as jnp
from jax import lax
from jax.experimental import pallas as pl
from jax.experimental.pallas import tpu as pltpu
from jax.sharding import PartitionSpec as P

KVH = 8
HD = 128
ROPE_BASE = 500000.0
EPS = 1e-05
VMEM_BYTES = 60 * 1024 * 1024


def swapped(value, axis, bit):
    mask = 2**bit
    pairs = [(source, source ^ mask) for source in range(lax.axis_size(axis))]
    return lax.ppermute(value, axis, pairs)


def rope_tables(positions):
    column = jnp.arange(HD, dtype=jnp.int32)
    within = (column - column % 2).astype(jnp.float32)
    inverse = jnp.exp(-(within / HD) * jnp.log(jnp.float32(ROPE_BASE)))
    angles = positions[:, None] * inverse[None, :]
    sign = jnp.where(column % 2 == 0, -1.0, 1.0)
    return jnp.cos(angles), jnp.sin(angles) * sign[None, :]


def turn(block, cosine, sine):
    lane = lax.broadcasted_iota(jnp.int32, block.shape, 1)
    neighbour = jnp.where(
        lane % 2 == 0, pltpu.roll(block, HD - 1, 1), pltpu.roll(block, 1, 1)
    )
    return block * cosine + neighbour * sine


def project_kernel(
    x_ref, gain_ref, wk_ref, wv_ref, cos_ref, sin_ref, pages_ref, heads_ref, key_acc, value_acc
):
    rows, width = x_ref.shape
    head_width = wk_ref.shape[1]
    depth = min(1024, width)
    steps = width // depth

    def squares(i, partial):
        chunk = x_ref[:, pl.ds(pl.multiple_of(i * depth, depth), depth)].astype(jnp.float32)
        chunk = chunk * chunk
        for j in range(depth // HD):
            partial = partial + chunk[:, j * HD : (j + 1) * HD]
        return partial

    partial = lax.fori_loop(0, steps, squares, jnp.zeros((rows, HD), jnp.float32))
    scale = lax.rsqrt(jnp.sum(partial, axis=1, keepdims=True) / width + EPS)
    key_acc[...] = jnp.zeros_like(key_acc)
    value_acc[...] = jnp.zeros_like(value_acc)

    def multiply(i, carry):
        part = pl.ds(pl.multiple_of(i * depth, depth), depth)
        normed = (x_ref[:, part].astype(jnp.float32) * scale * gain_ref[:, part]).astype(
            jnp.bfloat16
        )
        key_acc[...] += jnp.dot(normed, wk_ref[part, :], preferred_element_type=jnp.float32)
        value_acc[...] += jnp.dot(normed, wv_ref[part, :], preferred_element_type=jnp.float32)
        return carry

    lax.fori_loop(0, steps, multiply, 0)
    page = pages_ref.shape[2]
    for h in range(head_width // HD):
        cols = slice(h * HD, (h + 1) * HD)
        keys = turn(key_acc[:, cols], cos_ref[...], sin_ref[...]).astype(jnp.bfloat16)
        values = value_acc[:, cols].astype(jnp.bfloat16)
        heads_ref[h, 0] = keys
        heads_ref[h, 1] = values
        for b in range(rows // page):
            pages_ref[b, 0, :, cols] = keys[b * page : (b + 1) * page]
            pages_ref[b, 1, :, cols] = values[b * page : (b + 1) * page]


def project(x, gain, wk, wv, cosine, sine, page):
    tokens, width = x.shape
    head_width = wk.shape[1]
    heads = head_width // HD
    rows = min(256, tokens)
    return pl.pallas_call(
        project_kernel,
        grid=(tokens // rows,),
        in_specs=[
            pl.BlockSpec((rows, width), lambda i: (i, 0)),
            pl.BlockSpec((1, width), lambda i: (0, 0)),
            pl.BlockSpec((width, head_width), lambda i: (0, 0), pipeline_mode=pl.Buffered(1)),
            pl.BlockSpec((width, head_width), lambda i: (0, 0), pipeline_mode=pl.Buffered(1)),
            pl.BlockSpec((rows, HD), lambda i: (i, 0)),
            pl.BlockSpec((rows, HD), lambda i: (i, 0)),
        ],
        out_specs=[
            pl.BlockSpec((rows // page, 2, page, head_width), lambda i: (i, 0, 0, 0)),
            pl.BlockSpec((heads, 2, rows, HD), lambda i: (0, 0, i, 0)),
        ],
        out_shape=[
            jax.ShapeDtypeStruct((tokens // page, 2, page, head_width), jnp.bfloat16),
            jax.ShapeDtypeStruct((heads, 2, tokens, HD), jnp.bfloat16),
        ],
        scratch_shapes=[
            pltpu.VMEM((rows, head_width), jnp.float32),
            pltpu.VMEM((rows, head_width), jnp.float32),
        ],
        compiler_params=pltpu.CompilerParams(vmem_limit_bytes=VMEM_BYTES),
        cost_estimate=pl.CostEstimate(
            flops=4 * tokens * width * head_width,
            bytes_accessed=2 * tokens * width + 4 * width * head_width,
            transcendentals=0,
        ),
        name="project",
    )(x, gain, wk, wv, cosine, sine)


ROWS = 16


def attend_kernel(
    scalars, q_ref, new_ref, kv_ref, slot_row_ref, slot_col_ref, cos_ref, sin_ref, out_ref,
    rotated, acc, done,
):
    prompt, length = scalars[1], scalars[2]
    steps, requests, width = q_ref.shape
    group = width // HD
    sources, _, span, _ = kv_ref.shape
    rows = steps * group * ROWS
    score_scale = HD ** (-0.5)

    hit_row = slot_row_ref[...] == prompt
    hit_col = slot_col_ref[...] == prompt
    square = (requests, requests)
    first = lax.broadcasted_iota(jnp.int32, square, 0)
    second = lax.broadcasted_iota(jnp.int32, square, 1)
    rank_row = jnp.sum(
        jnp.where(hit_col & (first < second), 1.0, 0.0), axis=0, keepdims=True
    ).astype(jnp.int32)
    rank_col = jnp.sum(
        jnp.where(hit_row & (second < first), 1.0, 0.0), axis=1, keepdims=True
    ).astype(jnp.int32)
    count = jnp.sum(jnp.where(hit_row, 1.0, 0.0)).astype(jnp.int32)
    done[...] = jnp.zeros_like(done)
    chunks = (length + span - 1) // span

    def tile(k, carry):
        want = k * ROWS + lax.broadcasted_iota(jnp.int32, (ROWS, requests), 0)
        pick = jnp.where((rank_row == want) & hit_row, 1.0, 0.0).astype(jnp.bfloat16)
        fresh_keys, fresh_values = [], []
        for t in range(steps):
            cosine, sine = cos_ref[t : t + 1, :], sin_ref[t : t + 1, :]
            picked = jnp.dot(pick, q_ref[t], preferred_element_type=jnp.float32)
            for g in range(group):
                head = turn(picked[:, g * HD : (g + 1) * HD], cosine, sine)
                at = (t * group + g) * ROWS
                rotated[at : at + ROWS, :] = head.astype(jnp.bfloat16)
            picked = jnp.dot(pick, new_ref[0, t], preferred_element_type=jnp.float32)
            fresh_keys.append(turn(picked, cosine, sine).astype(jnp.bfloat16))
            picked = jnp.dot(pick, new_ref[1, t], preferred_element_type=jnp.float32)
            fresh_values.append(picked.astype(jnp.bfloat16))
        fresh_keys = jnp.concatenate(fresh_keys, axis=0)
        fresh_values = jnp.concatenate(fresh_values, axis=0)
        scores = score_scale * lax.dot_general(
            rotated[...], fresh_keys, (((1,), (1,)), ((), ())), preferred_element_type=jnp.float32
        )
        row = lax.broadcasted_iota(jnp.int32, scores.shape, 0)
        column = lax.broadcasted_iota(jnp.int32, scores.shape, 1)
        allowed = (row % ROWS == column % ROWS) & (column // ROWS <= row // (group * ROWS))
        peak = jnp.max(jnp.where(allowed, scores, -1e30), axis=1, keepdims=True)
        weights = jnp.where(allowed, jnp.exp(scores - peak), 0.0)
        total = jnp.sum(weights, axis=1, keepdims=True)
        acc[...] = jnp.dot(
            weights.astype(jnp.bfloat16), fresh_values, preferred_element_type=jnp.float32
        )

        def chunk(c, state):
            peak, total = state
            scores = score_scale * lax.dot_general(
                rotated[...], kv_ref[c, 0], (((1,), (1,)), ((), ())),
                preferred_element_type=jnp.float32,
            )
            position = c * span + lax.broadcasted_iota(jnp.int32, (1, span), 1)
            scores = jnp.where(position < length, scores, -1e30)
            new_peak = jnp.maximum(peak, jnp.max(scores, axis=1, keepdims=True))
            weights = jnp.exp(scores - new_peak)
            factor = jnp.exp(peak - new_peak)
            total = total * factor + jnp.sum(weights, axis=1, keepdims=True)
            acc[...] = acc[...] * factor + jnp.dot(
                weights.astype(jnp.bfloat16), kv_ref[c, 1], preferred_element_type=jnp.float32
            )
            return new_peak, total

        peak, total = lax.fori_loop(0, chunks, chunk, (peak, total))
        result = (acc[...] / total).astype(jnp.bfloat16)
        here = pl.ds(pl.multiple_of(k * ROWS, ROWS), ROWS)
        for t in range(steps):
            for g in range(group):
                at = (t * group + g) * ROWS
                done[t, here, g * HD : (g + 1) * HD] = result[at : at + ROWS]
        return carry

    lax.fori_loop(0, (count + ROWS - 1) // ROWS, tile, 0)
    place = jnp.where((rank_col == second) & hit_col, 1.0, 0.0).astype(jnp.bfloat16)
    owned = out_ref.shape[2]
    for t in range(steps):
        spread = jnp.dot(place, done[t], preferred_element_type=jnp.float32)
        for d in range(out_ref.shape[0]):
            out_ref[d, t] = spread[d * owned : (d + 1) * owned].astype(jnp.bfloat16)


def attend(scalars, queries, new_kv, kv, slots, cosine, sine, shards, seq_count, fresh_split):
    steps, requests, query_width = queries.shape
    width = query_width // seq_count
    rows = steps * (width // HD) * ROWS
    padded = -(-requests // ROWS) * ROWS
    whole = lambda shape: pl.BlockSpec(shape, lambda i, s: (0,) * len(shape))
    fresh_index = (lambda i, s: (0, 0, 0, s[0])) if fresh_split else (lambda i, s: (0, 0, 0, 0))
    return pl.pallas_call(
        attend_kernel,
        grid_spec=pltpu.PrefetchScalarGridSpec(
            num_scalar_prefetch=1,
            grid=(1,),
            in_specs=[
                pl.BlockSpec((steps, requests, width), lambda i, s: (0, 0, s[0])),
                pl.BlockSpec((2, steps, requests, HD), fresh_index),
                whole(kv.shape),
                whole((1, requests)),
                whole((requests, 1)),
                whole(cosine.shape),
                whole(sine.shape),
            ],
            out_specs=whole((shards, steps, requests // shards, width)),
            scratch_shapes=[
                pltpu.VMEM((rows, HD), jnp.bfloat16),
                pltpu.VMEM((rows, HD), jnp.float32),
                pltpu.VMEM((steps, padded, width), jnp.bfloat16),
            ],
        ),
        out_shape=jax.ShapeDtypeStruct(
            (shards, steps, requests // shards, width), jnp.bfloat16
        ),
        compiler_params=pltpu.CompilerParams(vmem_limit_bytes=VMEM_BYTES),
        cost_estimate=pl.CostEstimate(
            flops=steps * requests * width * kv.shape[0] * kv.shape[2],
            bytes_accessed=8 * 1024 * 1024,
            transcendentals=0,
        ),
        name="attend",
    )(scalars, queries, new_kv, kv, slots[None, :], slots[:, None], cosine, sine)


def body(
    prompt_x,
    norm_gain,
    key_weight,
    value_weight,
    prompt_lengths,
    page_table,
    request_slots,
    queries,
    new_kv,
):
    seq_count = lax.axis_size("seq")
    rep_count = lax.axis_size("rep")
    tp_count = lax.axis_size("tp")
    rep_index = lax.axis_index("rep")
    seq_index = lax.axis_index("seq")
    tp_index = lax.axis_index("tp")
    shard_index = rep_index * seq_count + seq_index
    shard_count = rep_count * seq_count
    tokens = prompt_x.shape[1]
    prompts, blocks_per_prompt = page_table.shape
    pages_here = blocks_per_prompt // seq_count
    page = tokens // pages_here
    copies = max(1, tp_count // KVH)
    key_cols, value_cols = key_weight, value_weight
    if tp_count > KVH:
        other_key, other_value = swapped((key_weight, value_weight), "tp", 0)
        low_half = tp_index % 2 == 0
        key_cols = jnp.where(
            low_half,
            jnp.concatenate([key_weight, other_key], 1),
            jnp.concatenate([other_key, key_weight], 1),
        )
        value_cols = jnp.where(
            low_half,
            jnp.concatenate([value_weight, other_value], 1),
            jnp.concatenate([other_value, value_weight], 1),
        )
    head_width = key_cols.shape[1]
    heads_here = head_width // HD
    head_start = tp_index * heads_here // copies

    own_new = lax.dynamic_slice_in_dim(new_kv, head_start * HD, head_width, 3)
    all_new = lax.all_gather(own_new, ("rep", "seq"), axis=2, tiled=True)

    token_pos = (seq_index * tokens + jnp.arange(tokens, dtype=jnp.int32)).astype(jnp.float32)
    cosine, sine = rope_tables(token_pos)
    pages, heads = project(
        prompt_x[0], norm_gain[None, :], key_cols, value_cols, cosine, sine, page
    )

    by_head = heads_here == seq_count
    if by_head:
        kv = lax.all_to_all(heads, "seq", split_axis=0, concat_axis=0, tiled=True)
    else:
        kv = lax.all_gather(heads, "seq", axis=0, tiled=True)

    own_pages = lax.dynamic_slice(page_table, (rep_index, seq_index * pages_here), (1, pages_here))[0]
    hits = (
        own_pages[None, :] // pages_here == jnp.arange(shard_count, dtype=jnp.int32)[:, None]
    ).astype(jnp.int32)
    chosen = jnp.sum(hits * jnp.arange(pages_here, dtype=jnp.int32)[None, :], axis=1)
    outgoing = jnp.take(pages, chosen, axis=0, mode="clip")
    arrived = lax.all_to_all(outgoing, ("rep", "seq"), split_axis=0, concat_axis=0, tiled=True)
    page_ids = shard_index * pages_here + jnp.arange(pages_here, dtype=jnp.int32)
    flat_source = jnp.arange(prompts * blocks_per_prompt, dtype=jnp.int32) // pages_here
    matches = (page_table.reshape(-1)[None, :] == page_ids[:, None]).astype(jnp.int32)
    sources = jnp.sum(matches * flat_source[None, :], axis=1)
    paged_cache = jnp.take(arrived, sources, axis=0, mode="clip")

    own_length = lax.dynamic_index_in_dim(prompt_lengths, rep_index, 0, keepdims=False)
    steps = queries.shape[0]
    step_pos = (own_length + jnp.arange(steps, dtype=jnp.int32)).astype(jnp.float32)
    step_cos, step_sin = rope_tables(step_pos)
    scalars = jnp.stack([seq_index, rep_index, own_length]).astype(jnp.int32)
    partial = attend(
        scalars, queries, all_new, kv, request_slots, step_cos, step_sin, shard_count, seq_count,
        by_head,
    )
    owned = lax.all_to_all(partial, ("rep", "seq"), split_axis=0, concat_axis=0, tiled=True)
    attention = jnp.concatenate(
        [
            functools.reduce(
                jnp.add, [owned[r * seq_count + s] for r in range(rep_count)]
            )
            for s in range(seq_count)
        ],
        axis=-1,
    )
    return (attention, paged_cache)


def solution(mesh):
    in_specs = (
        P("rep", "seq", None),
        P(),
        P(None, "tp"),
        P(None, "tp"),
        P(),
        P(),
        P(),
        P(None, None, "tp"),
        P(None, None, ("rep", "seq"), None),
    )
    out_specs = (P(None, ("rep", "seq"), "tp"), P(("rep", "seq"), None, None, "tp"))
    return jax.shard_map(body, mesh=mesh, in_specs=in_specs, out_specs=out_specs, check_vma=False)
```

profile of v0, /device:TPU:15, one launch (start us, length us, event | category | flops | bytes accessed | tf_op | source)
XLA Modules:
  0.0 236.4 jit_solution(17604666743328763545)
XLA Ops:
  7.2 0.8 copy-done
  8.1 0.6 constant_dynamic-slice_fusion
  8.8 3.1 %fusion = (f32[1024,128]{1,0:T(8,128)}, f32[1024,128]{1,0:T(8,128)}) fusion(f32[128]{0:T(128)S(1)} %get-tuple-element.14, f32[128]{0:T(128)S(1)} %get-tuple-element.15, f32[1024]{0:T(1024)S(1)} %add_convert_fusion), kind=kLoop, calls=%fused_computation.4 | loop fusion | flops 262144 | bytes 1053696 | tf_op jit(solution)/shard_map/mul | solution.py:29
  11.8 39.5 %project.1 = (bf16[8,2,128,512]{3,2,1,0:T(8,128)(2,1)}, bf16[4,2,1024,128]{3,2,1,0:T(8,128)(2,1)}) custom-call(bf16[1024,8192]{1,0:T(8,128)(2,1)} %bitcast.19, f32[1,8192]{1,0:T(1,128)} %bitcast.20, bf16[8192,512]{1,0:T(8,128)(2,1)} %wk_ref.1, bf16[8192,512]{1,0:T(8,128)(2,1)} %wv_ref.1, f32[1024,128]{1,0:T(8,128)} %get-tuple-element.11.cos_ref, ...), custom_call_target="tpu_custom_call" | custom-call | flops 17179869184 | bytes 33554432 | tf_op jit(solution)/shard_map/project/pallas_call | solution.py:87
  51.4 4.5 %all-to-all-start = ((bf16[4,2,1024,128]{3,2,1,0:T(8,128)(2,1)}), bf16[4,2,1024,128]{3,2,1,0:T(8,128)(2,1)S(1)}, u32[]{:S(2)}, u32[]{:S(2)}) async-start(bf16[4,2,1024,128]{3,2,1,0:T(8,128)(2,1)} %get-tuple-element.4), calls=%async_computation | async-start | bytes 4194304 | tf_op jit(solution)/shard_map/all_to_all | solution.py:308
  55.8 0.7 copy.12.slot_col_ref
  56.6 0.6 dynamic_slice.10
  57.2 0.6 add_convert_fusion.1
  57.9 1.3 pad_add_fusion.scalars
  59.2 0.7 fusion.5
  59.9 19.8 %all-to-all-done.kv_ref = bf16[4,2,1024,128]{3,2,1,0:T(8,128)(2,1)S(1)} async-done(((bf16[4,2,1024,128]{3,2,1,0:T(8,128)(2,1)}), bf16[4,2,1024,128]{3,2,1,0:T(8,128)(2,1)S(1)}, u32[]{:S(2)}, u32[]{:S(2)}) %all-to-all-start) | async-done | bytes 2097184 | tf_op jit(solution)/shard_map/all_to_all | solution.py:308
  79.7 1.3 copy-done.2
  81.0 13.7 %attend.1 = bf16[16,4,8,1024]{3,2,1,0:T(8,128)(2,1)} custom-call(s32[3]{0:T(128)} %pad_add_fusion.scalars, bf16[4,128,4096]{2,1,0:T(8,128)(2,1)} %q_ref.1, bf16[2,4,128,512]{3,2,1,0:T(8,128)(2,1)} %all-gather.2.cloned.1.call-done.new_ref, bf16[4,2,1024,128]{3,2,1,0:T(8,128)(2,1)} %copy-done.2, s32[1,128]{1,0:T(1,128)} %bitcast.17, ...), custom_call_target="tpu_custom_call" | custom-call | flops 2147483648 | bytes 8388608 | tf_op jit(solution)/shard_map/attend/pallas_call | solution.py:221
  94.7 8.5 %all-to-all-start.1 = ((bf16[16,4,8,1024]{3,2,1,0:T(8,128)(2,1)}), bf16[16,4,8,1024]{3,2,1,0:T(8,128)(2,1)S(1)}, u32[]{:S(2)}, u32[]{:S(2)}) async-start(bf16[16,4,8,1024]{3,2,1,0:T(8,128)(2,1)} %attend.1), calls=%async_computation.1 | async-start | bytes 2097152 | tf_op jit(solution)/shard_map/all_to_all | solution.py:334
  103.3 0.1 fusion.11
  103.3 0.1 select_reduce_fusion.1
  103.4 2.8 %gather_fusion = bf16[16,2,128,512]{3,2,1,0:T(8,128)(2,1)} fusion(bf16[8,2,128,512]{3,2,1,0:T(8,128)(2,1)S(1)} %copy-done.1, s32[1024]{0:T(1024)S(1)} %pad_clamp_fusion.1), kind=kCustom, calls=%fused_computation | custom fusion | bytes 8388672 | tf_op jit(solution)/shard_map/jit(_take)/gather | solution.py:317
  106.2 21.9 %all-to-all-done.1 = bf16[16,4,8,1024]{3,2,1,0:T(8,128)(2,1)S(1)} async-done(((bf16[16,4,8,1024]{3,2,1,0:T(8,128)(2,1)}), bf16[16,4,8,1024]{3,2,1,0:T(8,128)(2,1)S(1)}, u32[]{:S(2)}, u32[]{:S(2)}) %all-to-all-start.1) | async-done | bytes 1048608 | tf_op jit(solution)/shard_map/all_to_all | solution.py:334
  128.1 4.8 %all-to-all-start.2 = ((bf16[16,2,128,512]{3,2,1,0:T(8,128)(2,1)}), bf16[16,2,128,512]{3,2,1,0:T(8,128)(2,1)}, u32[]{:S(2)}, u32[]{:S(2)}) async-start(bf16[16,2,128,512]{3,2,1,0:T(8,128)(2,1)} %gather_fusion), calls=%async_computation.2 | async-start | bytes 8388608 | tf_op jit(solution)/shard_map/all_to_all | solution.py:318
  132.9 0.1 eq.50
  133.0 0.2 select_reduce_fusion
  133.3 0.7 pad_maximum_fusion
  134.0 91.4 %all-to-all-done.2 = bf16[16,2,128,512]{3,2,1,0:T(8,128)(2,1)} async-done(((bf16[16,2,128,512]{3,2,1,0:T(8,128)(2,1)}), bf16[16,2,128,512]{3,2,1,0:T(8,128)(2,1)}, u32[]{:S(2)}, u32[]{:S(2)}) %all-to-all-start.2) | async-done | bytes 4194336 | tf_op jit(solution)/shard_map/all_to_all | solution.py:318
  225.4 4.2 %gather_fusion.1 = bf16[8,2,128,512]{3,2,1,0:T(8,128)(2,1)} fusion(bf16[16,2,128,512]{3,2,1,0:T(8,128)(2,1)} %all-to-all-done.2, s32[1024]{0:T(1024)S(1)} %pad_clamp_fusion), kind=kCustom, calls=%fused_computation.1 | custom fusion | bytes 4194336 | tf_op jit(solution)/shard_map/jit(_take)/gather | solution.py:323
  (20 shorter events, 0.2 us)
Async XLA Ops:
  7.2 0.9 copy-start
  7.2 72.5 %all-gather.2.cloned.1.call-start = ((), (), s32[]{:S(2)}) async-start(), calls=%async_computation.3 | async-start | bytes 1114112 | tf_op jit(solution)/shard_map/all_gather | solution.py:298
  51.4 4.5 %copy-start.4 = (s32[128]{0:T(128)S(1)}, s32[128]{0:T(128)}, u32[]{:S(2)}) copy-start(s32[128]{0:T(128)} %param.15) | copy-start | bytes 1540
  51.4 5.2 %copy-start.5 = (s32[4]{0:T(128)S(1)}, s32[4]{0:T(128)}, u32[]{:S(2)}) copy-start(s32[4]{0:T(128)} %param.13) | copy-start | bytes 52
  51.4 28.3 %all-to-all-start = ((bf16[4,2,1024,128]{3,2,1,0:T(8,128)(2,1)}), bf16[4,2,1024,128]{3,2,1,0:T(8,128)(2,1)S(1)}, u32[]{:S(2)}, u32[]{:S(2)}) async-start(bf16[4,2,1024,128]{3,2,1,0:T(8,128)(2,1)} %get-tuple-element.4), calls=%async_computation | async-start | bytes 4194304 | tf_op jit(solution)/shard_map/all_to_all | solution.py:308
  79.7 1.3 copy-start.2
  81.0 22.3 %copy-start.3 = (s32[4,32]{1,0:T(4,128)S(1)}, s32[4,32]{1,0:T(4,128)}, u32[]{:S(2)}) copy-start(s32[4,32]{1,0:T(4,128)} %param.14) | copy-start | bytes 1540
  81.0 22.4 %copy-start.1 = (bf16[8,2,128,512]{3,2,1,0:T(8,128)(2,1)S(1)}, bf16[8,2,128,512]{3,2,1,0:T(8,128)(2,1)}, u32[]{:S(2)}) copy-start(bf16[8,2,128,512]{3,2,1,0:T(8,128)(2,1)} %get-tuple-element.5) | copy-start | bytes 6291460
  94.7 33.4 %all-to-all-start.1 = ((bf16[16,4,8,1024]{3,2,1,0:T(8,128)(2,1)}), bf16[16,4,8,1024]{3,2,1,0:T(8,128)(2,1)S(1)}, u32[]{:S(2)}, u32[]{:S(2)}) async-start(bf16[16,4,8,1024]{3,2,1,0:T(8,128)(2,1)} %attend.1), calls=%async_computation.1 | async-start | bytes 2097152 | tf_op jit(solution)/shard_map/all_to_all | solution.py:334
  128.1 97.3 %all-to-all-start.2 = ((bf16[16,2,128,512]{3,2,1,0:T(8,128)(2,1)}), bf16[16,2,128,512]{3,2,1,0:T(8,128)(2,1)}, u32[]{:S(2)}, u32[]{:S(2)}) async-start(bf16[16,2,128,512]{3,2,1,0:T(8,128)(2,1)} %gather_fusion), calls=%async_computation.2 | async-start | bytes 8388608 | tf_op jit(solution)/shard_map/all_to_all | solution.py:318
Sparse Core Ops, SparseCore 0:
  10.7 38.3 all-gather.1
where the time goes:
time: 238 us; the launch traced here: 236 us
  waiting for transfers between devices  133 us (56%)
  Pallas kernels  53.2 us (22%)
  starting transfers between devices  17.8 us (7%)
  between operations  14.1 us (6%)
  local copies, waits for them, and re-layouts  11.2 us (5%)
  other arithmetic  6.89 us (3%)
    all_to_all x1, waiting for transfers between devices, body(): lax.all_to_all(outgoing, ('rep', 'seq'), split_axis=0, concat_axis=0, til...  91.4 us
    pallas_call x1, Pallas kernels, project(): pl.pallas_call(project_kernel, grid=(tokens // rows,), in_specs=[pl.Block...  39.5 us
    all_to_all x1, waiting for transfers between devices, body(): lax.all_to_all(partial, ('rep', 'seq'), split_axis=0, concat_axis=0, tile...  21.9 us
    all_to_all x1, waiting for transfers between devices, body(): kv = lax.all_to_all(heads, 'seq', split_axis=0, concat_axis=0, tiled=True)  19.8 us
    pallas_call x1, Pallas kernels, attend(): pl.pallas_call(attend_kernel, grid_spec=pltpu.PrefetchScalarGridSpec(num_...  13.7 us
    all_to_all x1, starting transfers between devices, body(): lax.all_to_all(partial, ('rep', 'seq'), split_axis=0, concat_axis=0, tile...  8.53 us
    all_to_all x1, starting transfers between devices, body(): lax.all_to_all(outgoing, ('rep', 'seq'), split_axis=0, concat_axis=0, til...  4.8 us
  transfers between devices with their start and end apart: 4, of which 3 were waited for; matrix products, arithmetic and copies ran while one was open for 5% of the time, Pallas kernels for 17%

commit v1 on v0

--- a/solution.py
+++ b/solution.py
@@ -117,6 +117,432 @@
     )(x, gain, wk, wv, cosine, sine)
 
 
+MESH = pl.DeviceIdType.MESH
+
+
+def place_of(seq_count):
+    return lax.axis_index("rep") * seq_count + lax.axis_index("seq")
+
+
+def greet(shards, seq_count):
+    me = place_of(seq_count)
+    barrier = pltpu.get_barrier_semaphore()
+    for i in range(1, shards):
+        peer = lax.rem(me + i, shards)
+        pl.semaphore_signal(
+            barrier,
+            inc=1,
+            device_id={"rep": peer // seq_count, "seq": lax.rem(peer, seq_count)},
+            device_id_type=MESH,
+        )
+    pl.semaphore_wait(barrier, shards - 1)
+
+
+BLOCK = 256
+
+
+def stream_kernel(
+    shards, seq_count, x_hbm, gain_ref, wk_hbm, wv_hbm, page_cos, page_sin, cell_cos, cell_sin,
+    new_hbm, kv_out, new_out, xs, wide, acc, chunk, xsem, wsem, ksend, krecv, own_sem, nsend, nrecv,
+    nown,
+):
+    tokens, width = x_hbm.shape
+    heads = wk_hbm.shape[1] // HD
+    blocks = tokens // BLOCK
+    pairs = heads // 2
+    page = cell_cos.shape[0]
+    per_block = BLOCK // page
+    me = place_of(seq_count)
+    rep, seq = lax.axis_index("rep"), lax.axis_index("seq")
+    order = [(heads // 2 + k) % heads for k in range(heads)]
+    order = [o for o in order if o] + [0]
+    head_of = [lax.rem(seq + o, heads) for o in order]
+
+    def load_x(r):
+        return pltpu.make_async_copy(x_hbm.at[pl.ds(r * BLOCK, BLOCK)], xs.at[pl.ds(r * BLOCK, BLOCK)], xsem.at[r])
+
+    def load_w(k):
+        cols = pl.ds(pl.multiple_of(head_of[k] * HD, HD), HD)
+        at = (k % 2) * 2 * HD
+        return [
+            pltpu.make_async_copy(
+                w.at[:, cols], wide.at[k // 2, :, pl.ds(at + j * HD, HD)], wsem.at[k, j]
+            )
+            for j, w in enumerate((wk_hbm, wv_hbm))
+        ]
+
+    load_x(0).start()
+    for k in range(2):
+        for copy in load_w(k):
+            copy.start()
+    for r in range(1, blocks):
+        load_x(r).start()
+    for k in range(2, heads):
+        for copy in load_w(k):
+            copy.start()
+
+    greet(shards, seq_count)
+    owned = new_hbm.shape[2]
+    tp_head = lax.axis_index("tp") * heads
+
+    def new_copy(i):
+        peer = lax.rem(me + i, shards)
+        peer_seq = lax.rem(peer, seq_count)
+        cols = pl.ds(pl.multiple_of((tp_head + peer_seq) * HD, HD), HD)
+        return pltpu.make_async_remote_copy(
+            src_ref=new_hbm.at[:, :, :, cols],
+            dst_ref=new_out.at[:, :, pl.ds(pl.multiple_of(me * owned, owned), owned), :],
+            send_sem=nsend.at[i],
+            recv_sem=nrecv.at[i],
+            device_id={"rep": peer // seq_count, "seq": peer_seq},
+            device_id_type=MESH,
+        )
+
+    for i in range(1, shards):
+        new_copy(i).start()
+    own_new = pltpu.make_async_copy(
+        new_hbm.at[:, :, :, pl.ds(pl.multiple_of((tp_head + seq) * HD, HD), HD)],
+        new_out.at[:, :, pl.ds(pl.multiple_of(me * owned, owned), owned), :],
+        nown,
+    )
+    own_new.start()
+
+    sub = min(64, BLOCK)
+
+    def norm(r):
+        for q in range(r * BLOCK, (r + 1) * BLOCK, sub):
+            row = slice(q, q + sub)
+            partial = jnp.zeros((sub, HD), jnp.float32)
+            for j in range(0, width, 4 * HD):
+                piece = xs[row, j : j + 4 * HD].astype(jnp.float32)
+                piece = piece * piece
+                for s in range(4):
+                    partial = partial + piece[:, s * HD : (s + 1) * HD]
+            scale = lax.rsqrt(jnp.sum(partial, axis=1, keepdims=True) / width + EPS)
+            for j in range(0, width, 4 * HD):
+                cols = slice(j, j + 4 * HD)
+                xs[row, cols] = (
+                    xs[row, cols].astype(jnp.float32) * scale * gain_ref[:, cols]
+                ).astype(jnp.bfloat16)
+
+    def kv_copy(k, r):
+        part = pl.ds(r * per_block, per_block)
+        return pltpu.make_async_remote_copy(
+            src_ref=chunk.at[k, part],
+            dst_ref=kv_out.at[seq, part],
+            send_sem=ksend.at[k, r],
+            recv_sem=krecv.at[k, r],
+            device_id={"seq": head_of[k]},
+            device_id_type=MESH,
+        )
+
+    def own_copy(r):
+        part = pl.ds(r * per_block, per_block)
+        return pltpu.make_async_copy(
+            chunk.at[heads - 1, part], kv_out.at[seq, part], own_sem.at[r]
+        )
+
+    lane = lax.broadcasted_iota(jnp.int32, (page, HD), 1)
+    even = lane % 2 == 0
+
+    def finish(k, r, at):
+        for b in range(per_block):
+            rows = slice(b * page, (b + 1) * page)
+            n = r * per_block + b
+            base_cos, base_sin = page_cos[pl.ds(n, 1), :], page_sin[pl.ds(n, 1), :]
+            cosine = base_cos * cell_cos[...] - base_sin * cell_sin[...]
+            sine = base_sin * cell_cos[...] + base_cos * cell_sin[...]
+            keys = acc[rows, at : at + HD]
+            neighbour = jnp.where(even, -pltpu.roll(keys, HD - 1, 1), pltpu.roll(keys, 1, 1))
+            chunk[k, n, 0] = (keys * cosine + neighbour * sine).astype(jnp.bfloat16)
+            chunk[k, n, 1] = acc[rows, at + HD : at + 2 * HD].astype(jnp.bfloat16)
+        if k == heads - 1:
+            own_copy(r).start()
+        else:
+            kv_copy(k, r).start()
+
+    load_x(0).wait()
+    norm(0)
+    for k in range(2):
+        for copy in load_w(k):
+            copy.wait()
+    for r in range(blocks):
+        if r + 1 < blocks:
+            load_x(r + 1).wait()
+        acc[...] = jnp.dot(
+            xs[r * BLOCK : (r + 1) * BLOCK], wide[0], preferred_element_type=jnp.float32
+        )
+        if r + 1 < blocks:
+            norm(r + 1)
+        finish(0, r, 0)
+        finish(1, r, 2 * HD)
+    for pair in range(1, pairs):
+        for k in (2 * pair, 2 * pair + 1):
+            for copy in load_w(k):
+                copy.wait()
+
+        def rest(r, carry, pair=pair):
+            rows = pl.ds(pl.multiple_of(r * BLOCK, BLOCK), BLOCK)
+            acc[...] = jnp.dot(xs[rows], wide[pair], preferred_element_type=jnp.float32)
+            finish(2 * pair, r, 0)
+            finish(2 * pair + 1, r, 2 * HD)
+            return carry
+
+        lax.fori_loop(0, blocks, rest, 0)
+
+    for r in range(blocks):
+        own_copy(r).wait()
+        for k in range(heads - 1):
+            kv_copy(k, r).wait()
+    own_new.wait()
+    for i in range(1, shards):
+        new_copy(i).wait()
+
+
+def stream(x, gain, wk, wv, new_kv, page, shards, seq_count, seq_index):
+    tokens, width = x.shape
+    heads = wk.shape[1] // HD
+    blocks = tokens // BLOCK
+    pages = tokens // page
+    steps, owned = new_kv.shape[1:3]
+    first = (seq_index * pages + jnp.arange(pages, dtype=jnp.int32)) * page
+    page_cos, page_sin = angle_tables(first.astype(jnp.float32))
+    cell_cos, cell_sin = angle_tables(jnp.arange(page, dtype=jnp.int32).astype(jnp.float32))
+    anywhere = pl.BlockSpec(memory_space=pl.ANY)
+    here = pl.BlockSpec(memory_space=pltpu.VMEM)
+    return pl.pallas_call(
+        functools.partial(stream_kernel, shards, seq_count),
+        in_specs=[anywhere, here, anywhere, anywhere, here, here, here, here, anywhere],
+        out_specs=[anywhere, anywhere],
+        out_shape=[
+            jax.ShapeDtypeStruct((seq_count, pages, 2, page, HD), jnp.bfloat16),
+            jax.ShapeDtypeStruct((2, steps, shards * owned, HD), jnp.bfloat16),
+        ],
+        scratch_shapes=[
+            pltpu.VMEM((tokens, width), jnp.bfloat16),
+            pltpu.VMEM((heads // 2, width, 4 * HD), jnp.bfloat16),
+            pltpu.VMEM((BLOCK, 4 * HD), jnp.float32),
+            pltpu.VMEM((heads, pages, 2, page, HD), jnp.bfloat16),
+            pltpu.SemaphoreType.DMA((blocks,)),
+            pltpu.SemaphoreType.DMA((heads, 2)),
+            pltpu.SemaphoreType.DMA((heads, blocks)),
+            pltpu.SemaphoreType.DMA((heads, blocks)),
+            pltpu.SemaphoreType.DMA((blocks,)),
+            pltpu.SemaphoreType.DMA((shards,)),
+            pltpu.SemaphoreType.DMA((shards,)),
+            pltpu.SemaphoreType.DMA(()),
+        ],
+        compiler_params=pltpu.CompilerParams(
+            vmem_limit_bytes=VMEM_BYTES, collective_id=1, has_side_effects=True
+        ),
+        cost_estimate=pl.CostEstimate(
+            flops=4 * tokens * width * heads * HD,
+            bytes_accessed=2 * tokens * width + 4 * width * heads * HD,
+            transcendentals=0,
+        ),
+        name="stream",
+    )(x, gain, wk, wv, page_cos, page_sin, cell_cos, cell_sin, new_kv)
+
+
+def angle_tables(positions):
+    column = jnp.arange(HD, dtype=jnp.int32)
+    within = (column - column % 2).astype(jnp.float32)
+    inverse = jnp.exp(-(within / HD) * jnp.log(jnp.float32(ROPE_BASE)))
+    angles = positions[:, None] * inverse[None, :]
+    return jnp.cos(angles), jnp.sin(angles)
+
+
+PIECES = 4
+
+
+def exchange_kernel(
+    cap, seq_count, rep_count, send_ref, pick_ref, kv_hbm, part_ref, pages_out, attn_out,
+    kv, outgoing, turned, gathered, kv_sem, zsend, zrecv, psend, precv, psem, osend, orecv,
+    *landing,
+):
+    shards = seq_count * rep_count
+    blocks, _, page, _ = kv.shape
+    half = page // 2
+    pages = blocks // seq_count
+    rep, seq = lax.axis_index("rep"), lax.axis_index("seq")
+    me = place_of(seq_count)
+    load = pltpu.make_async_copy(kv_hbm, kv, kv_sem)
+    load.start()
+    greet(shards, seq_count)
+    load.wait()
+
+    def rows_of(k):
+        return k // 2, pl.ds((k % 2) * half, half)
+
+    def z_copy(k, d):
+        return pltpu.make_async_remote_copy(
+            src_ref=outgoing.at[k, d - 1],
+            dst_ref=landing[k].at[pl.ds((d - 1) * cap, cap)],
+            send_sem=zsend.at[k, d - 1],
+            recv_sem=zrecv.at[k, d - 1],
+            device_id={"rep": rep ^ d},
+            device_id_type=MESH,
+        )
+
+    far_first = sorted(range(1, rep_count), key=lambda d: -(d // 2 * 2))
+    for k in range(PIECES):
+        which, rows = rows_of(k)
+        for d in far_first:
+
+            def pack(j, carry, d=d, which=which, rows=rows, k=k):
+                outgoing[k, d - 1, j] = kv[send_ref[d, j], which, rows, :]
+                return carry
+
+            lax.fori_loop(0, cap, pack, 0)
+            z_copy(k, d).start()
+
+        def keep(j, carry, which=which, rows=rows, k=k):
+            landing[k][(rep_count - 1) * cap + j] = kv[send_ref[0, j], which, rows, :]
+            return carry
+
+        lax.fori_loop(0, landing[k].shape[0] - (rep_count - 1) * cap, keep, 0)
+
+    def part_copy(i):
+        peer = me ^ i
+        return pltpu.make_async_remote_copy(
+            src_ref=part_ref.at[peer],
+            dst_ref=gathered.at[me],
+            send_sem=osend.at[i],
+            recv_sem=orecv.at[i],
+            device_id={"rep": peer // seq_count, "seq": lax.rem(peer, seq_count)},
+            device_id_type=MESH,
+        )
+
+    for i in range(shards - 1, 0, -1):
+        part_copy(i).start()
+    gathered[me] = part_ref[me]
+
+    def p_copy(k, d):
+        which, rows = rows_of(k)
+        spot = pages_out.at[:, which, rows, pl.ds(pl.multiple_of(seq * HD, HD), HD)]
+        if d == 0:
+            return pltpu.make_async_copy(turned.at[k, 0], spot, psem.at[k])
+        return pltpu.make_async_remote_copy(
+            src_ref=turned.at[k, d],
+            dst_ref=spot,
+            send_sem=psend.at[k, d],
+            recv_sem=precv.at[k, d],
+            device_id={"seq": seq ^ d},
+            device_id_type=MESH,
+        )
+
+    for k in range(PIECES):
+        for d in far_first:
+            z_copy(k, d).wait()
+        for d in range(seq_count - 1, -1, -1):
+
+            def sort(j, carry, d=d, k=k):
+                turned[k, d, j] = landing[k][pick_ref[d, j]]
+                return carry
+
+            lax.fori_loop(0, pages, sort, 0)
+            p_copy(k, d).start()
+
+    for i in range(shards - 1, 0, -1):
+        part_copy(i).wait()
+    steps, owned, width = gathered.shape[1:]
+    for s in range(seq_count):
+        for t in range(steps):
+            total = gathered[s, t]
+            for z in range(1, rep_count):
+                total = total + gathered[z * seq_count + s, t]
+            attn_out[t, :, s * width : (s + 1) * width] = total
+
+    for k in range(PIECES):
+        for d in range(seq_count):
+            p_copy(k, d).wait()
+
+
+def exchange(cap, send, pick, kv, part, seq_count, rep_count, name, ident):
+    _, pages, _, page, _ = kv.shape
+    blocks = seq_count * pages
+    shards, steps, owned, width = part.shape
+    half = page // 2
+    anywhere = pl.BlockSpec(memory_space=pl.ANY)
+    here = pl.BlockSpec(memory_space=pltpu.VMEM)
+    numbers = pl.BlockSpec(memory_space=pltpu.SMEM)
+    landing = (rep_count - 1) * cap + send.shape[1]
+    sems = pltpu.SemaphoreType.DMA
+    return pl.pallas_call(
+        functools.partial(exchange_kernel, cap, seq_count, rep_count),
+        in_specs=[numbers, numbers, anywhere, here],
+        out_specs=[anywhere, here],
+        out_shape=[
+            jax.ShapeDtypeStruct((pages, 2, page, seq_count * HD), jnp.bfloat16),
+            jax.ShapeDtypeStruct((steps, owned, seq_count * width), jnp.bfloat16),
+        ],
+        scratch_shapes=[
+            pltpu.VMEM((blocks, 2, page, HD), jnp.bfloat16),
+            pltpu.VMEM((PIECES, rep_count - 1, cap, half, HD), jnp.bfloat16),
+            pltpu.VMEM((PIECES, seq_count, pages, half, HD), jnp.bfloat16),
+            pltpu.VMEM((shards, steps, owned, width), jnp.bfloat16),
+            sems(()),
+            sems((PIECES, rep_count)),
+            sems((PIECES, rep_count)),
+            sems((PIECES, seq_count)),
+            sems((PIECES, seq_count)),
+            sems((PIECES,)),
+            sems((shards,)),
+            sems((shards,)),
+        ]
+        + [pltpu.VMEM((landing, half, HD), jnp.bfloat16)] * PIECES,
+        compiler_params=pltpu.CompilerParams(
+            vmem_limit_bytes=VMEM_BYTES, collective_id=ident, has_side_effects=True
+        ),
+        cost_estimate=pl.CostEstimate(
+            flops=1, bytes_accessed=8 * 1024 * 1024, transcendentals=0
+        ),
+        name=name,
+    )(send, pick, kv.reshape(blocks, 2, page, HD), part)
+
+
+def routes(page_table, cap, rep_index, seq_index, rep_count, seq_count):
+    prompts, blocks = page_table.shape
+    pages = blocks // seq_count
+    most = blocks // 2
+    plane = page_table // (pages * seq_count)
+    block = jnp.arange(blocks, dtype=jnp.int32)
+    same = (plane[:, :, None] == plane[:, None, :]) & (block[None, :, None] > block[None, None, :])
+    rank = jnp.sum(same.astype(jnp.int32), axis=2)
+    apart = jnp.arange(rep_count, dtype=jnp.int32)
+    slot = jnp.arange(most, dtype=jnp.int32)
+    own_plane = lax.dynamic_index_in_dim(plane, rep_index, 0, keepdims=False)
+    own_rank = lax.dynamic_index_in_dim(rank, rep_index, 0, keepdims=False)
+    match = (own_plane[None, None, :] == (rep_index ^ apart)[:, None, None]) & (
+        own_rank[None, None, :] == slot[None, :, None]
+    )
+    send = jnp.sum(match.astype(jnp.int32) * block[None, None, :], axis=2)
+    away = jnp.arange(prompts, dtype=jnp.int32) ^ rep_index
+    origin = jnp.where(away == 0, (rep_count - 1), away - 1)
+    spot = (origin[:, None] * cap + rank).reshape(-1)
+    shard = rep_index * seq_count + (seq_index ^ jnp.arange(seq_count, dtype=jnp.int32))
+    wanted = shard[:, None] * pages + jnp.arange(pages, dtype=jnp.int32)[None, :]
+    found = (wanted[:, :, None] == page_table.reshape(-1)[None, None, :]).astype(jnp.int32)
+    pick = jnp.sum(found * spot[None, None, :], axis=2)
+    return send, pick
+
+
+def busiest(page_table, rep_count, seq_count):
+    prompts, blocks = page_table.shape
+    plane = page_table // blocks
+    counts = jnp.sum(
+        (plane[:, None, :] == jnp.arange(rep_count, dtype=jnp.int32)[None, :, None]).astype(
+            jnp.int32
+        ),
+        axis=2,
+    )
+    other = jnp.arange(prompts, dtype=jnp.int32)[:, None] != jnp.arange(rep_count)[None, :]
+    return jnp.max(jnp.where(other, counts, 0))
+
+
+TIGHT = 12
+
+
 ROWS = 16
 
 
@@ -127,7 +553,14 @@
     prompt, length = scalars[1], scalars[2]
     steps, requests, width = q_ref.shape
     group = width // HD
-    sources, _, span, _ = kv_ref.shape
+    paged = len(kv_ref.shape) == 5
+    span = kv_ref.shape[1] * kv_ref.shape[3] if paged else kv_ref.shape[2]
+
+    def source(c, which):
+        if paged:
+            return kv_ref[c, :, which].reshape(span, HD)
+        return kv_ref[c, which]
+
     rows = steps * group * ROWS
     score_scale = HD ** (-0.5)
 
@@ -179,7 +612,7 @@
         def chunk(c, state):
             peak, total = state
             scores = score_scale * lax.dot_general(
-                rotated[...], kv_ref[c, 0], (((1,), (1,)), ((), ())),
+                rotated[...], source(c, 0), (((1,), (1,)), ((), ())),
                 preferred_element_type=jnp.float32,
             )
             position = c * span + lax.broadcasted_iota(jnp.int32, (1, span), 1)
@@ -189,7 +622,7 @@
             factor = jnp.exp(peak - new_peak)
             total = total * factor + jnp.sum(weights, axis=1, keepdims=True)
             acc[...] = acc[...] * factor + jnp.dot(
-                weights.astype(jnp.bfloat16), kv_ref[c, 1], preferred_element_type=jnp.float32
+                weights.astype(jnp.bfloat16), source(c, 1), preferred_element_type=jnp.float32
             )
             return new_peak, total
 
@@ -244,12 +677,67 @@
         ),
         compiler_params=pltpu.CompilerParams(vmem_limit_bytes=VMEM_BYTES),
         cost_estimate=pl.CostEstimate(
-            flops=steps * requests * width * kv.shape[0] * kv.shape[2],
+            flops=steps * requests * width * kv.size // (2 * HD),
             bytes_accessed=8 * 1024 * 1024,
             transcendentals=0,
         ),
         name="attend",
     )(scalars, queries, new_kv, kv, slots[None, :], slots[:, None], cosine, sine)
+
+
+def fast_body(
+    prompt_x, norm_gain, key_weight, value_weight, prompt_lengths, page_table, request_slots,
+    queries, new_kv,
+):
+    seq_count = lax.axis_size("seq")
+    rep_count = lax.axis_size("rep")
+    rep_index = lax.axis_index("rep")
+    seq_index = lax.axis_index("seq")
+    shards = rep_count * seq_count
+    blocks = page_table.shape[1]
+    pages = blocks // seq_count
+    page = prompt_x.shape[1] // pages
+    kv, all_new = stream(
+        prompt_x[0], norm_gain[None, :], key_weight, value_weight, new_kv, page, shards,
+        seq_count, seq_index,
+    )
+    own_length = lax.dynamic_index_in_dim(prompt_lengths, rep_index, 0, keepdims=False)
+    steps = queries.shape[0]
+    step_pos = (own_length + jnp.arange(steps, dtype=jnp.int32)).astype(jnp.float32)
+    step_cos, step_sin = rope_tables(step_pos)
+    scalars = jnp.stack([seq_index, rep_index, own_length]).astype(jnp.int32)
+    part = attend(
+        scalars, queries, all_new, kv, request_slots, step_cos, step_sin, shards, seq_count, False
+    )
+    most = blocks // 2
+
+    def tight(args):
+        send, pick = routes(page_table, TIGHT, rep_index, seq_index, rep_count, seq_count)
+        return exchange(TIGHT, send, pick, *args, seq_count, rep_count, "exchange", 2)
+
+    def full(args):
+        send, pick = routes(page_table, most, rep_index, seq_index, rep_count, seq_count)
+        return exchange(most, send, pick, *args, seq_count, rep_count, "exchange_full", 3)
+
+    fits = busiest(page_table, rep_count, seq_count) <= TIGHT
+    paged_cache, attention = lax.cond(fits, tight, full, (kv, part))
+    return (attention, paged_cache)
+
+
+def quick(prompt_x, key_weight, page_table, new_kv):
+    seq_count, rep_count = lax.axis_size("seq"), lax.axis_size("rep")
+    heads = key_weight.shape[1] // HD
+    powers = all(n & (n - 1) == 0 for n in (seq_count, rep_count))
+    return (
+        powers
+        and key_weight.shape[1] % HD == 0
+        and heads == seq_count
+        and heads % 2 == 0
+        and lax.axis_size("tp") * heads == KVH
+        and prompt_x.shape[0] == 1
+        and page_table.shape[0] == rep_count
+        and prompt_x.shape[1] % BLOCK == 0
+    )
 
 
 def body(
@@ -272,6 +760,11 @@
     shard_index = rep_index * seq_count + seq_index
     shard_count = rep_count * seq_count
     tokens = prompt_x.shape[1]
+    if quick(prompt_x, key_weight, page_table, new_kv):
+        return fast_body(
+            prompt_x, norm_gain, key_weight, value_weight, prompt_lengths, page_table,
+            request_slots, queries, new_kv,
+        )
     prompts, blocks_per_prompt = page_table.shape
     pages_here = blocks_per_prompt // seq_count
     page = tokens // pages_here

time: 238 us -> 169 us (0.71)
  the two profiles are of different devices: /device:TPU:15 before, /device:TPU:0 now
where the time goes in v1:
time: 169 us; the launch traced here: 168 us
  Pallas kernels  152 us (90%)
  other arithmetic  7.81 us (5%)
  local copies, waits for them, and re-layouts  6.6 us (4%)
    pallas_call x1, Pallas kernels, exchange(): pl.pallas_call(functools.partial(exchange_kernel, cap, seq_count, rep_cou...  104 us
    pallas_call x1, Pallas kernels, stream(): pl.pallas_call(functools.partial(stream_kernel, shards, seq_count), in_sp...  39.3 us
    pallas_call x1, Pallas kernels, attend(): pl.pallas_call(attend_kernel, grid_spec=pltpu.PrefetchScalarGridSpec(num_...  8.73 us
    unnamed x4, local copies, waits for them, and re-layouts  3.81 us

profile of v1, /device:TPU:0, one launch (start us, length us, event | category | flops | bytes accessed | tf_op | source)
XLA Modules:
  0.0 167.8 jit_solution(15500132092090274537)
XLA Ops:
  0.6 1.2 dynamic_slice.21
  1.9 0.6 add_convert_fusion
  2.5 1.3 pad_add_fusion.scalars
  3.9 0.7 add_select_fusion.2
  4.6 0.1 convert_reduce_fusion.2
  4.7 0.6 select_reduce_fusion.4
  6.0 0.7 fusion.6
  6.7 0.7 multiply_sine_fusion.1
  7.4 1.4 copy.12.slot_col_ref
  8.8 1.0 multiply_sine_fusion
  9.7 39.3 %stream.1 = (bf16[4,8,2,128,128]{4,3,2,1,0:T(8,128)(2,1)S(1)}, bf16[2,4,128,128]{3,2,1,0:T(8,128)(2,1)}) custom-call(bf16[1024,8192]{1,0:T(8,128)(2,1)} %bitcast.21, f32[1,8192]{1,0:T(1,128)} %bitcast.22, bf16[8192,512]{1,0:T(8,128)(2,1)} %wk_hbm.1, bf16[8192,512]{1,0:T(8,128)(2,1)} %wv_hbm.1, f32[8,128]{1,0:T(8,128)} %get-tuple-element.53.page_cos, ...), custom_call_target="tpu_custom_call" | custom-call | flops 17179869184 | bytes 33554432 | tf_op jit(solution)/shard_map/stream/pallas_call | solution.py:313
  49.1 8.7 %attend.1 = bf16[16,4,8,1024]{3,2,1,0:T(8,128)(2,1)S(1)} custom-call(s32[3]{0:T(128)} %pad_add_fusion.scalars, bf16[4,128,4096]{2,1,0:T(8,128)(2,1)} %q_ref.1, bf16[2,4,128,128]{3,2,1,0:T(8,128)(2,1)} %get-tuple-element.37.new_ref, bf16[4,8,2,128,128]{4,3,2,1,0:T(8,128)(2,1)S(1)} %get-tuple-element.36.kv_ref, s32[1,128]{1,0:T(1,128)} %bitcast.20, ...), custom_call_target="tpu_custom_call" | custom-call | flops 2147483648 | bytes 8388608 | tf_op jit(solution)/shard_map/attend/pallas_call | solution.py:654
  57.8 106.1 %conditional.1 = ((bf16[8,2,128,512]{3,2,1,0:T(8,128)(2,1)}, bf16[4,8,4096]{2,1,0:T(8,128)(2,1)S(1)})) conditional(s32[]{:T(128)} %convert_element_type.55, (s32[4,32]{1,0:T(4,128)S(1)}, s32[]{:T(128)}, s32[]{:T(128)}, bf16[4,8,2,128,128]{4,3,2,1,0:T(8,128)(2,1)S(1)}, bf16[16,4,8,1024]{3,2,1,0:T(8,128)(2,1)S(1)}) %tuple.30, (s32[4,32]{1,0:T(4,128)S(1)}, ...), branch_computations={%region_2.6_spmd, %region_6.10_spmd} | conditional | flops 38377 | bytes 8399658 | solution.py:723
  57.8 0.1 eq.164
  58.0 0.1 iota_add_fusion.1
  58.0 0.2 convert_reduce_fusion.1
  58.3 0.1 broadcast_add_fusion.1
  58.3 0.1 add.146
  58.4 0.8 select_reduce_fusion.3.pick_ref
  59.2 0.1 broadcast_compare_fusion.1
  59.3 0.7 select_reduce_fusion.2.send_ref
  60.0 103.9 %exchange.1 = (bf16[8,2,128,512]{3,2,1,0:T(8,128)(2,1)}, bf16[4,8,4096]{2,1,0:T(8,128)(2,1)S(1)}) custom-call(s32[4,16]{1,0:T(4,128)} %select_reduce_fusion.2.send_ref, s32[4,8]{1,0:T(4,128)} %select_reduce_fusion.3.pick_ref, bf16[32,2,128,128]{3,2,1,0:T(8,128)(2,1)S(1)} %bitcast.18, bf16[16,4,8,1024]{3,2,1,0:T(8,128)(2,1)S(1)} %get-tuple-element.29.part_ref), custom_call_target="tpu_custom_call" | custom-call | flops 1 | bytes 8388608 | tf_op jit(solution)/shard_map/cond/branch_1_fun/exchange/pallas_call | solution.py:471
  164.0 0.7 copy.19
  164.7 3.1 %copy.20 = bf16[8,2,128,512]{3,2,1,0:T(8,128)(2,1)} copy(bf16[8,2,128,512]{3,2,1,0:T(8,128)(2,1)} %get-tuple-element.63) | data formatting | bytes 4194304
  (11 shorter events, 0.1 us)
Async XLA Ops:
  49.1 8.7 %copy-start = (s32[4,32]{1,0:T(4,128)S(1)}, s32[4,32]{1,0:T(4,128)}, u32[]{:S(2)}) copy-start(s32[4,32]{1,0:T(4,128)} %param.16) | copy-start | bytes 1540

commit v2 on v1

--- a/solution.py
+++ b/solution.py
@@ -139,10 +139,11 @@
 
 
 BLOCK = 256
+ROWS = 16
 
 
 def stream_kernel(
-    shards, seq_count, x_hbm, gain_ref, wk_hbm, wv_hbm, page_cos, page_sin, cell_cos, cell_sin,
+    shards, seq_count, page, x_hbm, gain_ref, wk_hbm, wv_hbm, cos_ref, sin_ref,
     new_hbm, kv_out, new_out, xs, wide, acc, chunk, xsem, wsem, ksend, krecv, own_sem, nsend, nrecv,
     nown,
 ):
@@ -150,7 +151,6 @@
     heads = wk_hbm.shape[1] // HD
     blocks = tokens // BLOCK
     pairs = heads // 2
-    page = cell_cos.shape[0]
     per_block = BLOCK // page
     me = place_of(seq_count)
     rep, seq = lax.axis_index("rep"), lax.axis_index("seq")
@@ -249,9 +249,10 @@
         for b in range(per_block):
             rows = slice(b * page, (b + 1) * page)
             n = r * per_block + b
-            base_cos, base_sin = page_cos[pl.ds(n, 1), :], page_sin[pl.ds(n, 1), :]
-            cosine = base_cos * cell_cos[...] - base_sin * cell_sin[...]
-            sine = base_sin * cell_cos[...] + base_cos * cell_sin[...]
+            base_cos, base_sin = cos_ref[pl.ds(page + n, 1), :], sin_ref[pl.ds(page + n, 1), :]
+            cell_cos, cell_sin = cos_ref[:page, :], sin_ref[:page, :]
+            cosine = base_cos * cell_cos - base_sin * cell_sin
+            sine = base_sin * cell_cos + base_cos * cell_sin
             keys = acc[rows, at : at + HD]
             neighbour = jnp.where(even, -pltpu.roll(keys, HD - 1, 1), pltpu.roll(keys, 1, 1))
             chunk[k, n, 0] = (keys * cosine + neighbour * sine).astype(jnp.bfloat16)
@@ -299,20 +300,17 @@
         new_copy(i).wait()
 
 
-def stream(x, gain, wk, wv, new_kv, page, shards, seq_count, seq_index):
+def stream(x, gain, wk, wv, new_kv, cosine, sine, page, shards, seq_count):
     tokens, width = x.shape
     heads = wk.shape[1] // HD
     blocks = tokens // BLOCK
     pages = tokens // page
     steps, owned = new_kv.shape[1:3]
-    first = (seq_index * pages + jnp.arange(pages, dtype=jnp.int32)) * page
-    page_cos, page_sin = angle_tables(first.astype(jnp.float32))
-    cell_cos, cell_sin = angle_tables(jnp.arange(page, dtype=jnp.int32).astype(jnp.float32))
     anywhere = pl.BlockSpec(memory_space=pl.ANY)
     here = pl.BlockSpec(memory_space=pltpu.VMEM)
     return pl.pallas_call(
-        functools.partial(stream_kernel, shards, seq_count),
-        in_specs=[anywhere, here, anywhere, anywhere, here, here, here, here, anywhere],
+        functools.partial(stream_kernel, shards, seq_count, page),
+        in_specs=[anywhere, here, anywhere, anywhere, here, here, anywhere],
         out_specs=[anywhere, anywhere],
         out_shape=[
             jax.ShapeDtypeStruct((seq_count, pages, 2, page, HD), jnp.bfloat16),
@@ -341,7 +339,7 @@
             transcendentals=0,
         ),
         name="stream",
-    )(x, gain, wk, wv, page_cos, page_sin, cell_cos, cell_sin, new_kv)
+    )(x, gain, wk, wv, cosine, sine, new_kv)
 
 
 def angle_tables(positions):
@@ -356,20 +354,32 @@
 
 
 def exchange_kernel(
-    cap, seq_count, rep_count, send_ref, pick_ref, kv_hbm, part_ref, pages_out, attn_out,
-    kv, outgoing, turned, gathered, kv_sem, zsend, zrecv, psend, precv, psem, osend, orecv,
-    *landing,
+    cap, seats, tiles, seq_count, rep_count, send_ref, pick_ref, length_ref, slot_ref, seat_ref,
+    cos_ref, sin_ref, kv_hbm, q_hbm, new_hbm, pages_out, attn_out,
+    kv, outgoing, turned, queries, fresh, rotated, acc, done, parts, landed, owned_out,
+    load_sem, zsend, zrecv, psend, precv, psem, osend, orecv, asend, arecv, asem, *landing,
 ):
     shards = seq_count * rep_count
     blocks, _, page, _ = kv.shape
     half = page // 2
     pages = blocks // seq_count
+    steps, requests, width = queries.shape
+    group = width // HD
     rep, seq = lax.axis_index("rep"), lax.axis_index("seq")
-    me = place_of(seq_count)
-    load = pltpu.make_async_copy(kv_hbm, kv, kv_sem)
-    load.start()
+    loads = [
+        pltpu.make_async_copy(kv_hbm, kv, load_sem.at[0]),
+        pltpu.make_async_copy(
+            q_hbm.at[:, :, pl.ds(pl.multiple_of(seq * width, width), width)],
+            queries,
+            load_sem.at[1],
+        ),
+        pltpu.make_async_copy(new_hbm, fresh, load_sem.at[2]),
+    ]
+    for load in loads:
+        load.start()
     greet(shards, seq_count)
-    load.wait()
+    for load in loads:
+        load.wait()
 
     def rows_of(k):
         return k // 2, pl.ds((k % 2) * half, half)
@@ -402,20 +412,111 @@
 
         lax.fori_loop(0, landing[k].shape[0] - (rep_count - 1) * cap, keep, 0)
 
-    def part_copy(i):
-        peer = me ^ i
+    length = length_ref[rep]
+    slot_row = slot_ref[...]
+    square = (requests, requests)
+    first = lax.broadcasted_iota(jnp.int32, square, 0)
+    second = lax.broadcasted_iota(jnp.int32, square, 1)
+    slot_col = jnp.sum(
+        jnp.where(first == second, slot_row.astype(jnp.float32), 0.0), axis=1, keepdims=True
+    )
+    hit_row = slot_row == rep
+    hit_col = slot_col == rep.astype(jnp.float32)
+    rank_row = jnp.sum(
+        jnp.where(hit_col & (first < second), 1.0, 0.0), axis=0, keepdims=True
+    ).astype(jnp.int32)
+    score_scale = HD ** (-0.5)
+    span = pages * page
+
+    def tile(k, carry):
+        want = k * ROWS + lax.broadcasted_iota(jnp.int32, (ROWS, requests), 0)
+        pick = jnp.where((rank_row == want) & hit_row, 1.0, 0.0).astype(jnp.bfloat16)
+        fresh_keys, fresh_values = [], []
+        for t in range(steps):
+            cosine, sine = cos_ref[t : t + 1, :], sin_ref[t : t + 1, :]
+            picked = jnp.dot(pick, queries[t], preferred_element_type=jnp.float32)
+            for g in range(group):
+                head = turn(picked[:, g * HD : (g + 1) * HD], cosine, sine)
+                at = (t * group + g) * ROWS
+                rotated[at : at + ROWS, :] = head.astype(jnp.bfloat16)
+            picked = jnp.dot(pick, fresh[0, t], preferred_element_type=jnp.float32)
+            fresh_keys.append(turn(picked, cosine, sine).astype(jnp.bfloat16))
+            picked = jnp.dot(pick, fresh[1, t], preferred_element_type=jnp.float32)
+            fresh_values.append(picked.astype(jnp.bfloat16))
+        fresh_keys = jnp.concatenate(fresh_keys, axis=0)
+        fresh_values = jnp.concatenate(fresh_values, axis=0)
+        scores = score_scale * lax.dot_general(
+            rotated[...], fresh_keys, (((1,), (1,)), ((), ())), preferred_element_type=jnp.float32
+        )
+        row = lax.broadcasted_iota(jnp.int32, scores.shape, 0)
+        column = lax.broadcasted_iota(jnp.int32, scores.shape, 1)
+        allowed = (row % ROWS == column % ROWS) & (column // ROWS <= row // (group * ROWS))
+        peak = jnp.max(jnp.where(allowed, scores, -1e30), axis=1, keepdims=True)
+        weights = jnp.where(allowed, jnp.exp(scores - peak), 0.0)
+        total = jnp.sum(weights, axis=1, keepdims=True)
+        acc[...] = jnp.dot(
+            weights.astype(jnp.bfloat16), fresh_values, preferred_element_type=jnp.float32
+        )
+
+        def chunk(c, state):
+            peak, total = state
+            part = pl.ds(pl.multiple_of(c * pages, pages), pages)
+            scores = score_scale * lax.dot_general(
+                rotated[...], kv[part, 0].reshape(span, HD), (((1,), (1,)), ((), ())),
+                preferred_element_type=jnp.float32,
+            )
+            position = c * span + lax.broadcasted_iota(jnp.int32, (1, span), 1)
+            scores = jnp.where(position < length, scores, -1e30)
+            new_peak = jnp.maximum(peak, jnp.max(scores, axis=1, keepdims=True))
+            weights = jnp.exp(scores - new_peak)
+            factor = jnp.exp(peak - new_peak)
+            total = total * factor + jnp.sum(weights, axis=1, keepdims=True)
+            acc[...] = acc[...] * factor + jnp.dot(
+                weights.astype(jnp.bfloat16), kv[part, 1].reshape(span, HD),
+                preferred_element_type=jnp.float32,
+            )
+            return new_peak, total
+
+        peak, total = lax.fori_loop(0, seq_count, chunk, (peak, total))
+        result = (acc[...] / total).astype(jnp.bfloat16)
+        here = pl.ds(pl.multiple_of(k * ROWS, ROWS), ROWS)
+        for t in range(steps):
+            for g in range(group):
+                at = (t * group + g) * ROWS
+                done[t, here, g * HD : (g + 1) * HD] = result[at : at + ROWS]
+        return carry
+
+    lax.fori_loop(0, tiles, tile, 0)
+
+    plane = requests // rep_count
+    packed = done.shape[1]
+    order = lax.broadcasted_iota(jnp.int32, (1, requests), 1)
+    spot = lax.broadcasted_iota(jnp.int32, (seats, packed), 0)
+    source = lax.broadcasted_iota(jnp.int32, (seats, packed), 1)
+
+    def o_copy(d):
+        rows = pl.ds(d * seats, seats)
         return pltpu.make_async_remote_copy(
-            src_ref=part_ref.at[peer],
-            dst_ref=gathered.at[me],
-            send_sem=osend.at[i],
-            recv_sem=orecv.at[i],
-            device_id={"rep": peer // seq_count, "seq": lax.rem(peer, seq_count)},
+            src_ref=parts.at[:, rows],
+            dst_ref=landed.at[:, rows],
+            send_sem=osend.at[d],
+            recv_sem=orecv.at[d],
+            device_id={"rep": rep ^ d},
             device_id_type=MESH,
         )
 
-    for i in range(shards - 1, 0, -1):
-        part_copy(i).start()
-    gathered[me] = part_ref[me]
+    for d in far_first + [0]:
+        begin = jnp.sum(
+            jnp.where(hit_row & (order < (rep ^ d) * plane), 1.0, 0.0), axis=1, keepdims=True
+        ).astype(jnp.int32)
+        moved = jnp.where(source == spot + begin, 1.0, 0.0).astype(jnp.bfloat16)
+        target = parts if d else landed
+        for t in range(steps):
+            target[t, d * seats : (d + 1) * seats] = jnp.dot(
+                moved, done[t], preferred_element_type=jnp.float32
+            ).astype(jnp.bfloat16)
+        if d:
+            o_copy(d).start()
 
     def p_copy(k, d):
         which, rows = rows_of(k)
@@ -443,52 +544,86 @@
             lax.fori_loop(0, pages, sort, 0)
             p_copy(k, d).start()
 
-    for i in range(shards - 1, 0, -1):
-        part_copy(i).wait()
-    steps, owned, width = gathered.shape[1:]
-    for s in range(seq_count):
-        for t in range(steps):
-            total = gathered[s, t]
-            for z in range(1, rep_count):
-                total = total + gathered[z * seq_count + s, t]
-            attn_out[t, :, s * width : (s + 1) * width] = total
-
+    owned = owned_out.shape[2]
+
+    def a_copy(d):
+        spot = attn_out.at[:, :, pl.ds(pl.multiple_of(seq * width, width), width)]
+        if d == 0:
+            return pltpu.make_async_copy(owned_out.at[seq], spot, asem)
+        return pltpu.make_async_remote_copy(
+            src_ref=owned_out.at[seq ^ d],
+            dst_ref=spot,
+            send_sem=asend.at[d],
+            recv_sem=arecv.at[d],
+            device_id={"seq": seq ^ d},
+            device_id_type=MESH,
+        )
+
+    for d in far_first:
+        o_copy(d).wait()
+    chosen = lax.broadcasted_iota(jnp.int32, (plane, rep_count * seats), 1) == seat_ref[...]
+    chosen = jnp.where(chosen, 1.0, 0.0).astype(jnp.bfloat16)
+    for t in range(steps):
+        spread = jnp.dot(chosen, landed[t], preferred_element_type=jnp.float32)
+        for s in range(seq_count):
+            owned_out[s, t] = spread[s * owned : (s + 1) * owned].astype(jnp.bfloat16)
+    for d in range(seq_count - 1, -1, -1):
+        a_copy(d).start()
     for k in range(PIECES):
         for d in range(seq_count):
             p_copy(k, d).wait()
-
-
-def exchange(cap, send, pick, kv, part, seq_count, rep_count, name, ident):
+    for d in range(seq_count):
+        a_copy(d).wait()
+
+
+def exchange(
+    cap, seats, tiles, tables, lengths, slots, seat, cosine, sine, kv, queries, fresh, seq_count,
+    rep_count, name, ident,
+):
+    send, pick = tables
     _, pages, _, page, _ = kv.shape
     blocks = seq_count * pages
-    shards, steps, owned, width = part.shape
+    steps, requests, query_width = queries.shape
+    width = query_width // seq_count
+    rows = steps * (width // HD) * ROWS
     half = page // 2
+    owned = requests // (rep_count * seq_count)
     anywhere = pl.BlockSpec(memory_space=pl.ANY)
     here = pl.BlockSpec(memory_space=pltpu.VMEM)
     numbers = pl.BlockSpec(memory_space=pltpu.SMEM)
     landing = (rep_count - 1) * cap + send.shape[1]
     sems = pltpu.SemaphoreType.DMA
     return pl.pallas_call(
-        functools.partial(exchange_kernel, cap, seq_count, rep_count),
-        in_specs=[numbers, numbers, anywhere, here],
-        out_specs=[anywhere, here],
+        functools.partial(exchange_kernel, cap, seats, tiles, seq_count, rep_count),
+        in_specs=[numbers] * 3 + [here] * 4 + [anywhere] * 3,
+        out_specs=[anywhere, anywhere],
         out_shape=[
             jax.ShapeDtypeStruct((pages, 2, page, seq_count * HD), jnp.bfloat16),
-            jax.ShapeDtypeStruct((steps, owned, seq_count * width), jnp.bfloat16),
+            jax.ShapeDtypeStruct((steps, owned, query_width), jnp.bfloat16),
         ],
         scratch_shapes=[
             pltpu.VMEM((blocks, 2, page, HD), jnp.bfloat16),
             pltpu.VMEM((PIECES, rep_count - 1, cap, half, HD), jnp.bfloat16),
             pltpu.VMEM((PIECES, seq_count, pages, half, HD), jnp.bfloat16),
-            pltpu.VMEM((shards, steps, owned, width), jnp.bfloat16),
-            sems(()),
+            pltpu.VMEM((steps, requests, width), jnp.bfloat16),
+            pltpu.VMEM(fresh.shape, jnp.bfloat16),
+            pltpu.VMEM((rows, HD), jnp.bfloat16),
+            pltpu.VMEM((rows, HD), jnp.float32),
+            pltpu.VMEM((steps, tiles * ROWS, width), jnp.bfloat16),
+            pltpu.VMEM((steps, rep_count * seats, width), jnp.bfloat16),
+            pltpu.VMEM((steps, rep_count * seats, width), jnp.bfloat16),
+            pltpu.VMEM((seq_count, steps, owned, width), jnp.bfloat16),
+            sems((3,)),
             sems((PIECES, rep_count)),
             sems((PIECES, rep_count)),
             sems((PIECES, seq_count)),
             sems((PIECES, seq_count)),
             sems((PIECES,)),
-            sems((shards,)),
-            sems((shards,)),
+            sems((rep_count,)),
+            sems((rep_count,)),
+            sems((seq_count,)),
+            sems((seq_count,)),
+            sems(()),
         ]
         + [pltpu.VMEM((landing, half, HD), jnp.bfloat16)] * PIECES,
         compiler_params=pltpu.CompilerParams(
@@ -498,7 +633,10 @@
             flops=1, bytes_accessed=8 * 1024 * 1024, transcendentals=0
         ),
         name=name,
-    )(send, pick, kv.reshape(blocks, 2, page, HD), part)
+    )(
+        send, pick, lengths, slots[None, :], seat, cosine, sine,
+        kv.reshape(blocks, 2, page, HD), queries, fresh,
+    )
 
 
 def routes(page_table, cap, rep_index, seq_index, rep_count, seq_count):
@@ -527,23 +665,34 @@
     return send, pick
 
 
-def busiest(page_table, rep_count, seq_count):
+def seat_rows(request_slots, seats, rep_index, rep_count):
+    plane = request_slots.shape[0] // rep_count
+    mine = lax.dynamic_slice_in_dim(request_slots, rep_index * plane, plane, 0)
+    index = jnp.arange(plane, dtype=jnp.int32)
+    before = (mine[:, None] == mine[None, :]) & (index[None, :] < index[:, None])
+    return (mine ^ rep_index)[:, None] * seats + jnp.sum(
+        before.astype(jnp.int32), axis=1, keepdims=True
+    )
+
+
+def fits(page_table, request_slots, tiles, rep_count):
     prompts, blocks = page_table.shape
+    each = jnp.arange(rep_count, dtype=jnp.int32)
     plane = page_table // blocks
-    counts = jnp.sum(
-        (plane[:, None, :] == jnp.arange(rep_count, dtype=jnp.int32)[None, :, None]).astype(
-            jnp.int32
-        ),
-        axis=2,
-    )
-    other = jnp.arange(prompts, dtype=jnp.int32)[:, None] != jnp.arange(rep_count)[None, :]
-    return jnp.max(jnp.where(other, counts, 0))
+    counts = jnp.sum((plane[:, None, :] == each[None, :, None]).astype(jnp.int32), axis=2)
+    other = jnp.arange(prompts, dtype=jnp.int32)[:, None] != each[None, :]
+    by_plane = request_slots.reshape(rep_count, -1)
+    asked = jnp.sum((by_plane[None, :, :] == each[:, None, None]).astype(jnp.int32), axis=2)
+    return (
+        jnp.all((counts <= TIGHT) | ~other)
+        & jnp.all(asked <= SEATS)
+        & jnp.all(jnp.sum(asked, axis=1) <= tiles * ROWS)
+    )
 
 
 TIGHT = 12
-
-
-ROWS = 16
+SEATS = 16
+TILES = 4
 
 
 def attend_kernel(
@@ -697,30 +846,49 @@
     blocks = page_table.shape[1]
     pages = blocks // seq_count
     page = prompt_x.shape[1] // pages
+    steps, requests, _ = queries.shape
+    own_length = prompt_lengths[0]
+    for r in range(1, rep_count):
+        own_length = jnp.where(rep_index == r, prompt_lengths[r], own_length)
+    index = jnp.arange(page + pages + 8, dtype=jnp.int32)
+    positions = jnp.where(
+        index < page,
+        index,
+        jnp.where(
+            index < page + pages,
+            (seq_index * pages + index - page) * page,
+            own_length + index - page - pages,
+        ),
+    )
+    cosine, sine = angle_tables(positions.astype(jnp.float32))
     kv, all_new = stream(
-        prompt_x[0], norm_gain[None, :], key_weight, value_weight, new_kv, page, shards,
-        seq_count, seq_index,
-    )
-    own_length = lax.dynamic_index_in_dim(prompt_lengths, rep_index, 0, keepdims=False)
-    steps = queries.shape[0]
-    step_pos = (own_length + jnp.arange(steps, dtype=jnp.int32)).astype(jnp.float32)
-    step_cos, step_sin = rope_tables(step_pos)
-    scalars = jnp.stack([seq_index, rep_index, own_length]).astype(jnp.int32)
-    part = attend(
-        scalars, queries, all_new, kv, request_slots, step_cos, step_sin, shards, seq_count, False
+        prompt_x[0], norm_gain[None, :], key_weight, value_weight, new_kv, cosine, sine, page,
+        shards, seq_count,
     )
     most = blocks // 2
-
-    def tight(args):
-        send, pick = routes(page_table, TIGHT, rep_index, seq_index, rep_count, seq_count)
-        return exchange(TIGHT, send, pick, *args, seq_count, rep_count, "exchange", 2)
-
-    def full(args):
-        send, pick = routes(page_table, most, rep_index, seq_index, rep_count, seq_count)
-        return exchange(most, send, pick, *args, seq_count, rep_count, "exchange_full", 3)
-
-    fits = busiest(page_table, rep_count, seq_count) <= TIGHT
-    paged_cache, attention = lax.cond(fits, tight, full, (kv, part))
+    plane = requests // rep_count
+    sign = jnp.where(jnp.arange(HD, dtype=jnp.int32) % 2 == 0, -1.0, 1.0)
+    first = page + pages
+    step_cos, step_sin = cosine[first : first + steps], sine[first : first + steps] * sign
+
+    def route(cap, seats, tiles, name, ident):
+        tables = routes(page_table, cap, rep_index, seq_index, rep_count, seq_count)
+        seat = seat_rows(request_slots, seats, rep_index, rep_count)
+
+        def run(args):
+            return exchange(
+                cap, seats, tiles, tables, prompt_lengths, request_slots, seat, step_cos,
+                step_sin, *args, seq_count, rep_count, name, ident,
+            )
+
+        return run
+
+    paged_cache, attention = lax.cond(
+        fits(page_table, request_slots, TILES, rep_count),
+        route(TIGHT, SEATS, TILES, "exchange", 2),
+        route(most, plane, -(-requests // ROWS), "exchange_full", 3),
+        (kv, queries, all_new),
+    )
     return (attention, paged_cache)
 
 
@@ -737,6 +905,7 @@
         and prompt_x.shape[0] == 1
         and page_table.shape[0] == rep_count
         and prompt_x.shape[1] % BLOCK == 0
+        and new_kv.shape[2] * seq_count * rep_count % (rep_count * ROWS) == 0
     )
 
 

time: 169 us -> 147 us (0.87)
  the two profiles are of different devices: /device:TPU:0 before, /device:TPU:15 now
where the time goes in v2:
time: 147 us; the launch traced here: 146 us
  Pallas kernels  127 us (86%)
  local copies, waits for them, and re-layouts  8.21 us (6%)
  between operations  5.27 us (4%)
  other arithmetic  5.05 us (3%)
    pallas_call x1, Pallas kernels, exchange(): pl.pallas_call(functools.partial(exchange_kernel, cap, seats, tiles, seq_...  90.6 us
    pallas_call x1, Pallas kernels, stream(): pl.pallas_call(functools.partial(stream_kernel, shards, seq_count, page),...  36.3 us
    unnamed x10, local copies, waits for them, and re-layouts  4.43 us

profile of v2, /device:TPU:15, one launch (start us, length us, event | category | flops | bytes accessed | tf_op | source)
XLA Modules:
  0.0 145.7 jit_solution(3716821766927344472)
XLA Ops:
  0.7 0.8 eq.194
  1.4 0.7 broadcast_xor_fusion
  2.2 0.2 convert_reduce_fusion.1
  2.4 0.1 broadcast_compare_fusion
  2.5 0.7 add_select_fusion
  3.2 0.1 convert_reduce_fusion.4
  3.3 0.7 eq.85
  4.1 0.2 convert_reduce_fusion.2
  4.3 0.7 fusion.7
  6.3 0.6 compare_reduce_fusion
  7.6 1.5 %fusion.14 = (s32[1]{0:T(128)}, s32[1]{0:T(128)}, s32[1]{0:T(128)}, s32[1]{0:T(128)}) fusion(s32[4]{0:T(128)} %param.15), kind=kLoop, calls=%fused_computation.59 | loop fusion | bytes 32 | tf_op jit(solution)/shard_map/slice | solution.py:850
  11.6 0.2 convert_reduce_fusion
  11.8 0.1 broadcast_compare_fusion.1
  11.9 0.2 select_reduce_fusion.2
  12.1 0.3 multiply_sine_fusion
  12.5 0.6 copy-done
  13.1 36.3 %stream.1 = (bf16[4,8,2,128,128]{4,3,2,1,0:T(8,128)(2,1)S(1)}, bf16[2,4,128,128]{3,2,1,0:T(8,128)(2,1)S(1)}) custom-call(bf16[1024,8192]{1,0:T(8,128)(2,1)} %bitcast.22, f32[1,8192]{1,0:T(1,128)} %bitcast.23, bf16[8192,512]{1,0:T(8,128)(2,1)} %wk_hbm.1, bf16[8192,512]{1,0:T(8,128)(2,1)} %wv_hbm.1, f32[144,128]{1,0:T(8,128)} %copy-done.1, ...), custom_call_target="tpu_custom_call" | custom-call | flops 17179869184 | bytes 33554432 | tf_op jit(solution)/shard_map/stream/pallas_call | solution.py:311
  49.4 92.5 %conditional.1 = ((bf16[8,2,128,512]{3,2,1,0:T(8,128)(2,1)}, bf16[4,8,4096]{2,1,0:T(8,128)(2,1)S(1)})) conditional(s32[]{:T(128)} %convert_element_type.37, (s32[128]{0:T(128)S(1)}, bf16[4,8,2,128,128]{4,3,2,1,0:T(8,128)(2,1)S(1)}, s32[4,16]{1,0:T(4,128)S(1)}, pred[4,8,128]{2,1,0:T(8,128)(4,1)S(1)}, s32[4]{0:T(128)S(1)}, ...), branch_computations={%region_11.12_spmd, %region_12.13_spmd} | conditional | flops 8357 | bytes 8412484 | solution.py:886
  49.7 0.1 add.178
  49.8 0.7 select_reduce_fusion.1.pick_ref
  50.5 0.7 copy.14.seat_ref
  51.2 90.6 %exchange.1 = (bf16[8,2,128,512]{3,2,1,0:T(8,128)(2,1)}, bf16[4,8,4096]{2,1,0:T(8,128)(2,1)S(1)}) custom-call(s32[4,16]{1,0:T(4,128)S(1)} %get-tuple-element.50.send_ref, s32[4,8]{1,0:T(4,128)} %select_reduce_fusion.1.pick_ref, s32[4]{0:T(128)S(1)} %get-tuple-element.52.length_ref, s32[1,128]{1,0:T(1,128)S(1)} %bitcast.21, s32[32,1]{1,0:T(8,128)} %copy.14.seat_ref, ...), custom_call_target="tpu_custom_call" | custom-call | flops 1 | bytes 8388608 | tf_op jit(solution)/shard_map/cond/branch_1_fun/exchange/pallas_call | solution.py:596
  141.9 0.7 copy.21
  142.6 3.1 %copy.22 = bf16[8,2,128,512]{3,2,1,0:T(8,128)(2,1)} copy(bf16[8,2,128,512]{3,2,1,0:T(8,128)(2,1)} %get-tuple-element.133) | data formatting | bytes 4194304
  (21 shorter events, 0.3 us)
Async XLA Ops:
  12.4 0.6 copy-start
  12.4 0.6 copy-start.1
  13.1 36.3 %copy-start.2 = (s32[4]{0:T(128)S(1)}, s32[4]{0:T(128)}, u32[]{:S(2)}) copy-start(s32[4]{0:T(128)} %param.15) | copy-start | bytes 52
  13.1 36.3 %copy-start.3 = (s32[128]{0:T(128)S(1)}, s32[128]{0:T(128)}, u32[]{:S(2)}) copy-start(s32[128]{0:T(128)} %param.17) | copy-start | bytes 1540

commit v3 on v2

--- a/solution.py
+++ b/solution.py
@@ -2,6 +2,7 @@
 
 import jax
 import jax.numpy as jnp
+import numpy as np
 from jax import lax
 from jax.experimental import pallas as pl
 from jax.experimental.pallas import tpu as pltpu
@@ -138,13 +139,91 @@
     pl.semaphore_wait(barrier, shards - 1)
 
 
+TIGHT = 12
+SEATS = 16
+TILES = 4
+ROWS = 16
+
+
+def power(n):
+    return n.bit_length() - 1
+
+
+def plan(table_ref, slot_ref, plan_out, rep_count, seq_count, rep, seq):
+    prompts, blocks = table_ref.shape
+    pages = blocks // seq_count
+    most = blocks // 2
+    requests = slot_ref.shape[1]
+    table = table_ref[...].astype(jnp.float32)
+    plane = jnp.floor(table * (1.0 / blocks))
+    square = (blocks, blocks)
+    above = lax.broadcasted_iota(jnp.int32, square, 0)
+    across = lax.broadcasted_iota(jnp.int32, square, 1)
+    index = lax.broadcasted_iota(jnp.int32, (blocks, 1), 0)
+    shard = rep * seq_count + (seq ^ (index >> power(pages)))
+    wanted = (shard * pages + (index & (pages - 1))).astype(jnp.float32)
+    small = jnp.zeros((blocks, 1), jnp.float32)
+    large = jnp.zeros((blocks, 1), jnp.float32)
+    own_plane = jnp.zeros((1, blocks), jnp.float32)
+    own_rank = jnp.zeros((1, blocks), jnp.float32)
+    worst = jnp.zeros((1, 1), jnp.float32)
+    for p in range(prompts):
+        row = plane[p : p + 1, :]
+        col = jnp.sum(jnp.where(above == across, row, 0.0), axis=1, keepdims=True)
+        rank = jnp.sum(
+            jnp.where((col == row) & (above < across), 1.0, 0.0), axis=0, keepdims=True
+        )
+        own_plane = own_plane + jnp.where(rep == p, row, 0.0)
+        own_rank = own_rank + jnp.where(rep == p, rank, 0.0)
+        away = rep ^ p
+        origin = jnp.where(away == 0, rep_count - 1, away - 1).astype(jnp.float32)
+        found = table[p : p + 1, :] == wanted
+        small = small + jnp.sum(
+            jnp.where(found, rank + origin * TIGHT, 0.0), axis=1, keepdims=True
+        )
+        large = large + jnp.sum(jnp.where(found, rank + origin * most, 0.0), axis=1, keepdims=True)
+        for z in range(rep_count):
+            if z != p:
+                count = jnp.sum(jnp.where(row == z, 1.0, 0.0), axis=1, keepdims=True)
+                worst = jnp.maximum(worst, count)
+    slots = slot_ref[...]
+    owner = lax.broadcasted_iota(jnp.int32, (1, requests), 1) >> power(requests // rep_count)
+    asked = jnp.zeros((1, 1), jnp.float32)
+    packed = jnp.zeros((1, 1), jnp.float32)
+    for p in range(prompts):
+        every = jnp.zeros((1, 1), jnp.float32)
+        for z in range(rep_count):
+            count = jnp.sum(
+                jnp.where((slots == p) & (owner == z), 1.0, 0.0), axis=1, keepdims=True
+            )
+            asked = jnp.maximum(asked, count)
+            every = every + count
+        packed = jnp.maximum(packed, every)
+    enough = (worst <= TIGHT) & (asked <= SEATS) & (packed <= TILES * ROWS)
+    lanes = lax.broadcasted_iota(jnp.int32, (blocks, HD), 1)
+    plan_out[:blocks] = jnp.where(
+        lanes == 0, small, jnp.where(lanes == 1, large, 0.0)
+    ).astype(jnp.int32)
+    step = lax.broadcasted_iota(jnp.int32, (most, blocks), 0).astype(jnp.float32)
+    number = lax.broadcasted_iota(jnp.int32, (most, blocks), 1).astype(jnp.float32)
+    lanes = lax.broadcasted_iota(jnp.int32, (most, HD), 1)
+    send = jnp.zeros((most, HD), jnp.float32)
+    for d in range(rep_count):
+        goal = (rep ^ d).astype(jnp.float32)
+        match = (own_plane == goal) & (own_rank == step)
+        column = jnp.sum(jnp.where(match, number, 0.0), axis=1, keepdims=True)
+        send = send + jnp.where(lanes == d, column, 0.0)
+    plan_out[blocks : blocks + most] = send.astype(jnp.int32)
+    flag = jnp.where(enough, 1.0, 0.0) + jnp.zeros((8, HD), jnp.float32)
+    plan_out[blocks + most :] = flag.astype(jnp.int32)
+
+
 BLOCK = 256
-ROWS = 16
 
 
 def stream_kernel(
-    shards, seq_count, page, x_hbm, gain_ref, wk_hbm, wv_hbm, cos_ref, sin_ref,
-    new_hbm, kv_out, new_out, xs, wide, acc, chunk, xsem, wsem, ksend, krecv, own_sem, nsend, nrecv,
+    shards, seq_count, page, length_ref, x_hbm, gain_ref, wk_hbm, wv_hbm, inverse_ref, table_ref,
+    slot_ref, new_hbm, kv_out, new_out, plan_out, step_out, row_cos, row_sin, xs, wide, acc, chunk, xsem, wsem, ksend, krecv, own_sem, nsend, nrecv,
     nown,
 ):
     tokens, width = x_hbm.shape
@@ -206,6 +285,28 @@
         nown,
     )
     own_new.start()
+
+    plan(table_ref, slot_ref, plan_out, shards // seq_count, seq_count, rep, seq)
+    count = tokens // page
+    inverse = inverse_ref[...]
+    cells = lax.broadcasted_iota(jnp.int32, (page, HD), 0)
+    bases = (seq * count + lax.broadcasted_iota(jnp.int32, (count, HD), 0)) * page
+    later = length_ref[rep] + lax.broadcasted_iota(jnp.int32, (8, HD), 0)
+    cell_angle = cells.astype(jnp.float32) * inverse
+    base_angle = bases.astype(jnp.float32) * inverse
+    step_angle = later.astype(jnp.float32) * inverse
+    cell_cos, cell_sin = jnp.cos(cell_angle), jnp.sin(cell_angle)
+    page_cos, page_sin = jnp.cos(base_angle), jnp.sin(base_angle)
+    even_row = lax.broadcasted_iota(jnp.int32, (1, HD), 1) % 2 == 0
+    step_sin = jnp.sin(step_angle)
+    step_out[:8] = jnp.cos(step_angle)
+    step_out[8:] = jnp.where(even_row, -step_sin, step_sin)
+    for n in range(tokens // page):
+        rows = slice(n * page, (n + 1) * page)
+        base_cos, base_sin = page_cos[n : n + 1], page_sin[n : n + 1]
+        row_cos[rows] = base_cos * cell_cos - base_sin * cell_sin
+        sine = base_sin * cell_cos + base_cos * cell_sin
+        row_sin[rows] = jnp.where(even_row, -sine, sine)
 
     sub = min(64, BLOCK)
 
@@ -249,13 +350,12 @@
         for b in range(per_block):
             rows = slice(b * page, (b + 1) * page)
             n = r * per_block + b
-            base_cos, base_sin = cos_ref[pl.ds(page + n, 1), :], sin_ref[pl.ds(page + n, 1), :]
-            cell_cos, cell_sin = cos_ref[:page, :], sin_ref[:page, :]
-            cosine = base_cos * cell_cos - base_sin * cell_sin
-            sine = base_sin * cell_cos + base_cos * cell_sin
+            here = pl.ds(pl.multiple_of(n * page, page), page)
             keys = acc[rows, at : at + HD]
-            neighbour = jnp.where(even, -pltpu.roll(keys, HD - 1, 1), pltpu.roll(keys, 1, 1))
-            chunk[k, n, 0] = (keys * cosine + neighbour * sine).astype(jnp.bfloat16)
+            neighbour = jnp.where(even, pltpu.roll(keys, HD - 1, 1), pltpu.roll(keys, 1, 1))
+            chunk[k, n, 0] = (keys * row_cos[here] + neighbour * row_sin[here]).astype(
+                jnp.bfloat16
+            )
             chunk[k, n, 1] = acc[rows, at + HD : at + 2 * HD].astype(jnp.bfloat16)
         if k == heads - 1:
             own_copy(r).start()
@@ -270,13 +370,16 @@
     for r in range(blocks):
         if r + 1 < blocks:
             load_x(r + 1).wait()
+        if r:
+            finish(0, r - 1, 0)
+            finish(1, r - 1, 2 * HD)
         acc[...] = jnp.dot(
             xs[r * BLOCK : (r + 1) * BLOCK], wide[0], preferred_element_type=jnp.float32
         )
         if r + 1 < blocks:
             norm(r + 1)
-        finish(0, r, 0)
-        finish(1, r, 2 * HD)
+    finish(0, blocks - 1, 0)
+    finish(1, blocks - 1, 2 * HD)
     for pair in range(1, pairs):
         for k in (2 * pair, 2 * pair + 1):
             for copy in load_w(k):
@@ -300,23 +403,33 @@
         new_copy(i).wait()
 
 
-def stream(x, gain, wk, wv, new_kv, cosine, sine, page, shards, seq_count):
+def stream(
+    x, gain, wk, wv, new_kv, lengths, page_table, slots, page, shards, seq_count
+):
     tokens, width = x.shape
     heads = wk.shape[1] // HD
     blocks = tokens // BLOCK
     pages = tokens // page
     steps, owned = new_kv.shape[1:3]
+    column = np.arange(HD)
+    within = (column - column % 2) / HD
+    inverse = jnp.asarray(np.exp(-within * np.log(ROPE_BASE))[None, :], jnp.float32)
     anywhere = pl.BlockSpec(memory_space=pl.ANY)
     here = pl.BlockSpec(memory_space=pltpu.VMEM)
     return pl.pallas_call(
         functools.partial(stream_kernel, shards, seq_count, page),
-        in_specs=[anywhere, here, anywhere, anywhere, here, here, anywhere],
-        out_specs=[anywhere, anywhere],
+        in_specs=[pl.BlockSpec(memory_space=pltpu.SMEM)]
+        + [anywhere, here, anywhere, anywhere, here, here, here, anywhere],
+        out_specs=[anywhere, anywhere, here, here],
         out_shape=[
             jax.ShapeDtypeStruct((seq_count, pages, 2, page, HD), jnp.bfloat16),
             jax.ShapeDtypeStruct((2, steps, shards * owned, HD), jnp.bfloat16),
+            jax.ShapeDtypeStruct((seq_count * pages * 3 // 2 + 8, HD), jnp.int32),
+            jax.ShapeDtypeStruct((16, HD), jnp.float32),
         ],
         scratch_shapes=[
+            pltpu.VMEM((tokens, HD), jnp.float32),
+            pltpu.VMEM((tokens, HD), jnp.float32),
             pltpu.VMEM((tokens, width), jnp.bfloat16),
             pltpu.VMEM((heads // 2, width, 4 * HD), jnp.bfloat16),
             pltpu.VMEM((BLOCK, 4 * HD), jnp.float32),
@@ -339,23 +452,15 @@
             transcendentals=0,
         ),
         name="stream",
-    )(x, gain, wk, wv, cosine, sine, new_kv)
-
-
-def angle_tables(positions):
-    column = jnp.arange(HD, dtype=jnp.int32)
-    within = (column - column % 2).astype(jnp.float32)
-    inverse = jnp.exp(-(within / HD) * jnp.log(jnp.float32(ROPE_BASE)))
-    angles = positions[:, None] * inverse[None, :]
-    return jnp.cos(angles), jnp.sin(angles)
+    )(lengths, x, gain, wk, wv, inverse, page_table, slots[None, :], new_kv)
 
 
 PIECES = 4
 
 
 def exchange_kernel(
-    cap, seats, tiles, seq_count, rep_count, send_ref, pick_ref, length_ref, slot_ref, seat_ref,
-    cos_ref, sin_ref, kv_hbm, q_hbm, new_hbm, pages_out, attn_out,
+    cap, seats, tiles, lane, seq_count, rep_count, plan_ref, length_ref, slot_ref,
+    turn_ref, kv_hbm, q_hbm, new_hbm, pages_out, attn_out,
     kv, outgoing, turned, queries, fresh, rotated, acc, done, parts, landed, owned_out,
     load_sem, zsend, zrecv, psend, precv, psem, osend, orecv, asend, arecv, asem, *landing,
 ):
@@ -400,14 +505,14 @@
         for d in far_first:
 
             def pack(j, carry, d=d, which=which, rows=rows, k=k):
-                outgoing[k, d - 1, j] = kv[send_ref[d, j], which, rows, :]
+                outgoing[k, d - 1, j] = kv[plan_ref[blocks + j, d], which, rows, :]
                 return carry
 
             lax.fori_loop(0, cap, pack, 0)
             z_copy(k, d).start()
 
         def keep(j, carry, which=which, rows=rows, k=k):
-            landing[k][(rep_count - 1) * cap + j] = kv[send_ref[0, j], which, rows, :]
+            landing[k][(rep_count - 1) * cap + j] = kv[plan_ref[blocks + j, 0], which, rows, :]
             return carry
 
         lax.fori_loop(0, landing[k].shape[0] - (rep_count - 1) * cap, keep, 0)
@@ -433,7 +538,7 @@
         pick = jnp.where((rank_row == want) & hit_row, 1.0, 0.0).astype(jnp.bfloat16)
         fresh_keys, fresh_values = [], []
         for t in range(steps):
-            cosine, sine = cos_ref[t : t + 1, :], sin_ref[t : t + 1, :]
+            cosine, sine = turn_ref[t : t + 1, :], turn_ref[8 + t : 9 + t, :]
             picked = jnp.dot(pick, queries[t], preferred_element_type=jnp.float32)
             for g in range(group):
                 head = turn(picked[:, g * HD : (g + 1) * HD], cosine, sine)
@@ -538,7 +643,7 @@
         for d in range(seq_count - 1, -1, -1):
 
             def sort(j, carry, d=d, k=k):
-                turned[k, d, j] = landing[k][pick_ref[d, j]]
+                turned[k, d, j] = landing[k][plan_ref[d * pages + j, lane]]
                 return carry
 
             lax.fori_loop(0, pages, sort, 0)
@@ -561,7 +666,16 @@
 
     for d in far_first:
         o_copy(d).wait()
-    chosen = lax.broadcasted_iota(jnp.int32, (plane, rep_count * seats), 1) == seat_ref[...]
+    wide = (plane, requests)
+    number = lax.broadcasted_iota(jnp.int32, wide, 1)
+    mine = rep * plane + lax.broadcasted_iota(jnp.int32, wide, 0)
+    prompt = jnp.sum(
+        jnp.where(number == mine, slot_row.astype(jnp.float32), 0.0), axis=1, keepdims=True
+    )
+    ahead = (slot_row.astype(jnp.float32) == prompt) & (number >= rep * plane) & (number < mine)
+    seat = jnp.sum(jnp.where(ahead, 1.0, 0.0), axis=1, keepdims=True).astype(jnp.int32)
+    seat = seat + (prompt.astype(jnp.int32) ^ rep) * seats
+    chosen = lax.broadcasted_iota(jnp.int32, (plane, rep_count * seats), 1) == seat
     chosen = jnp.where(chosen, 1.0, 0.0).astype(jnp.bfloat16)
     for t in range(steps):
         spread = jnp.dot(chosen, landed[t], preferred_element_type=jnp.float32)
@@ -577,10 +691,9 @@
 
 
 def exchange(
-    cap, seats, tiles, tables, lengths, slots, seat, cosine, sine, kv, queries, fresh, seq_count,
+    cap, seats, tiles, lane, table, lengths, slots, turns, kv, queries, fresh, seq_count,
     rep_count, name, ident,
 ):
-    send, pick = tables
     _, pages, _, page, _ = kv.shape
     blocks = seq_count * pages
     steps, requests, query_width = queries.shape
@@ -591,11 +704,11 @@
     anywhere = pl.BlockSpec(memory_space=pl.ANY)
     here = pl.BlockSpec(memory_space=pltpu.VMEM)
     numbers = pl.BlockSpec(memory_space=pltpu.SMEM)
-    landing = (rep_count - 1) * cap + send.shape[1]
+    landing = (rep_count - 1) * cap + blocks // 2
     sems = pltpu.SemaphoreType.DMA
     return pl.pallas_call(
-        functools.partial(exchange_kernel, cap, seats, tiles, seq_count, rep_count),
-        in_specs=[numbers] * 3 + [here] * 4 + [anywhere] * 3,
+        functools.partial(exchange_kernel, cap, seats, tiles, lane, seq_count, rep_count),
+        in_specs=[numbers] * 2 + [here] * 2 + [anywhere] * 3,
         out_specs=[anywhere, anywhere],
         out_shape=[
             jax.ShapeDtypeStruct((pages, 2, page, seq_count * HD), jnp.bfloat16),
@@ -634,65 +747,9 @@
         ),
         name=name,
     )(
-        send, pick, lengths, slots[None, :], seat, cosine, sine,
+        table, lengths, slots[None, :], turns,
         kv.reshape(blocks, 2, page, HD), queries, fresh,
     )
-
-
-def routes(page_table, cap, rep_index, seq_index, rep_count, seq_count):
-    prompts, blocks = page_table.shape
-    pages = blocks // seq_count
-    most = blocks // 2
-    plane = page_table // (pages * seq_count)
-    block = jnp.arange(blocks, dtype=jnp.int32)
-    same = (plane[:, :, None] == plane[:, None, :]) & (block[None, :, None] > block[None, None, :])
-    rank = jnp.sum(same.astype(jnp.int32), axis=2)
-    apart = jnp.arange(rep_count, dtype=jnp.int32)
-    slot = jnp.arange(most, dtype=jnp.int32)
-    own_plane = lax.dynamic_index_in_dim(plane, rep_index, 0, keepdims=False)
-    own_rank = lax.dynamic_index_in_dim(rank, rep_index, 0, keepdims=False)
-    match = (own_plane[None, None, :] == (rep_index ^ apart)[:, None, None]) & (
-        own_rank[None, None, :] == slot[None, :, None]
-    )
-    send = jnp.sum(match.astype(jnp.int32) * block[None, None, :], axis=2)
-    away = jnp.arange(prompts, dtype=jnp.int32) ^ rep_index
-    origin = jnp.where(away == 0, (rep_count - 1), away - 1)
-    spot = (origin[:, None] * cap + rank).reshape(-1)
-    shard = rep_index * seq_count + (seq_index ^ jnp.arange(seq_count, dtype=jnp.int32))
-    wanted = shard[:, None] * pages + jnp.arange(pages, dtype=jnp.int32)[None, :]
-    found = (wanted[:, :, None] == page_table.reshape(-1)[None, None, :]).astype(jnp.int32)
-    pick = jnp.sum(found * spot[None, None, :], axis=2)
-    return send, pick
-
-
-def seat_rows(request_slots, seats, rep_index, rep_count):
-    plane = request_slots.shape[0] // rep_count
-    mine = lax.dynamic_slice_in_dim(request_slots, rep_index * plane, plane, 0)
-    index = jnp.arange(plane, dtype=jnp.int32)
-    before = (mine[:, None] == mine[None, :]) & (index[None, :] < index[:, None])
-    return (mine ^ rep_index)[:, None] * seats + jnp.sum(
-        before.astype(jnp.int32), axis=1, keepdims=True
-    )
-
-
-def fits(page_table, request_slots, tiles, rep_count):
-    prompts, blocks = page_table.shape
-    each = jnp.arange(rep_count, dtype=jnp.int32)
-    plane = page_table // blocks
-    counts = jnp.sum((plane[:, None, :] == each[None, :, None]).astype(jnp.int32), axis=2)
-    other = jnp.arange(prompts, dtype=jnp.int32)[:, None] != each[None, :]
-    by_plane = request_slots.reshape(rep_count, -1)
-    asked = jnp.sum((by_plane[None, :, :] == each[:, None, None]).astype(jnp.int32), axis=2)
-    return (
-        jnp.all((counts <= TIGHT) | ~other)
-        & jnp.all(asked <= SEATS)
-        & jnp.all(jnp.sum(asked, axis=1) <= tiles * ROWS)
-    )
-
-
-TIGHT = 12
-SEATS = 16
-TILES = 4
 
 
 def attend_kernel(
@@ -840,53 +897,30 @@
 ):
     seq_count = lax.axis_size("seq")
     rep_count = lax.axis_size("rep")
-    rep_index = lax.axis_index("rep")
-    seq_index = lax.axis_index("seq")
     shards = rep_count * seq_count
     blocks = page_table.shape[1]
     pages = blocks // seq_count
     page = prompt_x.shape[1] // pages
     steps, requests, _ = queries.shape
-    own_length = prompt_lengths[0]
-    for r in range(1, rep_count):
-        own_length = jnp.where(rep_index == r, prompt_lengths[r], own_length)
-    index = jnp.arange(page + pages + 8, dtype=jnp.int32)
-    positions = jnp.where(
-        index < page,
-        index,
-        jnp.where(
-            index < page + pages,
-            (seq_index * pages + index - page) * page,
-            own_length + index - page - pages,
-        ),
-    )
-    cosine, sine = angle_tables(positions.astype(jnp.float32))
-    kv, all_new = stream(
-        prompt_x[0], norm_gain[None, :], key_weight, value_weight, new_kv, cosine, sine, page,
-        shards, seq_count,
+    kv, all_new, table, turns = stream(
+        prompt_x[0], norm_gain[None, :], key_weight, value_weight, new_kv, prompt_lengths,
+        page_table, request_slots, page, shards, seq_count,
     )
     most = blocks // 2
     plane = requests // rep_count
-    sign = jnp.where(jnp.arange(HD, dtype=jnp.int32) % 2 == 0, -1.0, 1.0)
-    first = page + pages
-    step_cos, step_sin = cosine[first : first + steps], sine[first : first + steps] * sign
-
-    def route(cap, seats, tiles, name, ident):
-        tables = routes(page_table, cap, rep_index, seq_index, rep_count, seq_count)
-        seat = seat_rows(request_slots, seats, rep_index, rep_count)
-
+    def route(cap, seats, tiles, lane, name, ident):
         def run(args):
             return exchange(
-                cap, seats, tiles, tables, prompt_lengths, request_slots, seat, step_cos,
-                step_sin, *args, seq_count, rep_count, name, ident,
+                cap, seats, tiles, lane, table, prompt_lengths, request_slots, turns, *args, seq_count,
+                rep_count, name, ident,
             )
 
         return run
 
     paged_cache, attention = lax.cond(
-        fits(page_table, request_slots, TILES, rep_count),
-        route(TIGHT, SEATS, TILES, "exchange", 2),
-        route(most, plane, -(-requests // ROWS), "exchange_full", 3),
+        table[blocks + most, 0] > 0,
+        route(TIGHT, SEATS, TILES, 0, "exchange", 2),
+        route(most, plane, -(-requests // ROWS), 1, "exchange_full", 3),
         (kv, queries, all_new),
     )
     return (attention, paged_cache)
@@ -895,9 +929,13 @@
 def quick(prompt_x, key_weight, page_table, new_kv):
     seq_count, rep_count = lax.axis_size("seq"), lax.axis_size("rep")
     heads = key_weight.shape[1] // HD
-    powers = all(n & (n - 1) == 0 for n in (seq_count, rep_count))
+    powers = all(
+        n & (n - 1) == 0 for n in (seq_count, rep_count, new_kv.shape[2] * seq_count)
+    )
     return (
         powers
+        and page_table.shape[1] & (page_table.shape[1] - 1) == 0
+        and page_table.shape[1] % (2 * seq_count) == 0
         and key_weight.shape[1] % HD == 0
         and heads == seq_count
         and heads % 2 == 0
@@ -905,6 +943,7 @@
         and prompt_x.shape[0] == 1
         and page_table.shape[0] == rep_count
         and prompt_x.shape[1] % BLOCK == 0
+        and new_kv.shape[1] <= 8
         and new_kv.shape[2] * seq_count * rep_count % (rep_count * ROWS) == 0
     )
 

time: 147 us -> 134 us (0.912)
  other arithmetic: 5.05 us -> 0 us
  between operations: 5.27 us -> 1.34 us
  local copies, waits for them, and re-layouts: 8.21 us -> 4.32 us
    reduce_sum x6 -> x0, other arithmetic: 1.65 us -> none  [the longest x1 0.73 us: routes(): pick = jnp.sum(found * spot[None, None, :], axis=2)]
    eq x2 -> x0, local copies, waits for them, and re-layouts: 1.51 us -> none  [the longest x1 0.77 us: routes(): wanted[:, :, None] == page_table.reshape(-1)[None, None, :]]
    unnamed x10 -> x6, local copies, waits for them, and re-layouts: 4.43 us -> 3.81 us
where the time goes in v3:
time: 134 us; the launch traced here: 132 us
  Pallas kernels  127 us (95%)
  local copies, waits for them, and re-layouts  4.32 us (3%)
  between operations  1.34 us (1%)
    pallas_call x1, Pallas kernels, exchange(): pl.pallas_call(functools.partial(exchange_kernel, cap, seats, tiles, lane...  90.3 us
    pallas_call x1, Pallas kernels, stream(): pl.pallas_call(functools.partial(stream_kernel, shards, seq_count, page),...  36.3 us
    unnamed x6, local copies, waits for them, and re-layouts  3.81 us

profile of v3, /device:TPU:15, one launch (start us, length us, event | category | flops | bytes accessed | tf_op | source)
XLA Modules:
  0.0 132.2 jit_solution(12161479422474267091)
XLA Ops:
  0.6 0.0 copy-start
  0.6 0.0 copy-start.1
  0.7 36.3 %stream.1 = (bf16[4,8,2,128,128]{4,3,2,1,0:T(8,128)(2,1)S(1)}, bf16[2,4,128,128]{3,2,1,0:T(8,128)(2,1)S(1)}, s32[56,128]{1,0:T(8,128)S(1)}, f32[16,128]{1,0:T(8,128)S(1)}) custom-call(s32[4]{0:T(128)} %length_ref.1, bf16[1024,8192]{1,0:T(8,128)(2,1)} %bitcast.13, f32[1,8192]{1,0:T(1,128)} %bitcast.14, bf16[8192,512]{1,0:T(8,128)(2,1)} %wk_hbm.1, ...), custom_call_target="tpu_custom_call" | custom-call | flops 17179869184 | bytes 33554432 | tf_op jit(solution)/shard_map/stream/pallas_call | solution.py:419
  36.9 0.5 slice.3
  38.1 0.0 copy-done
  38.1 0.0 copy-done.1
  38.1 90.3 %conditional.1 = ((bf16[8,2,128,512]{3,2,1,0:T(8,128)(2,1)}, bf16[4,8,4096]{2,1,0:T(8,128)(2,1)S(1)})) conditional(s32[]{:T(128)} %bitcast.7, (s32[128]{0:T(128)S(1)}, bf16[4,8,2,128,128]{4,3,2,1,0:T(8,128)(2,1)S(1)}, s32[56,128]{1,0:T(8,128)S(1)}, s32[4]{0:T(128)S(1)}, f32[16,128]{1,0:T(8,128)S(1)}, /*index=5*/bf16[4,128,4096]{2,1,0:T(8,128)(2,1)}, ...), branch_computations={%region_0.0_spmd, %region_1.0_spmd} | conditional | flops 1 | bytes 8388616 | solution.py:920
  38.1 90.3 %exchange.1 = (bf16[8,2,128,512]{3,2,1,0:T(8,128)(2,1)}, bf16[4,8,4096]{2,1,0:T(8,128)(2,1)S(1)}) custom-call(s32[56,128]{1,0:T(8,128)S(1)} %get-tuple-element.35.plan_ref, s32[4]{0:T(128)S(1)} %get-tuple-element.36.length_ref, s32[1,128]{1,0:T(1,128)S(1)} %bitcast.12, f32[16,128]{1,0:T(8,128)S(1)} %get-tuple-element.38.turn_ref, ...), custom_call_target="tpu_custom_call" | custom-call | flops 1 | bytes 8388608 | tf_op jit(solution)/shard_map/cond/branch_1_fun/exchange/pallas_call | solution.py:709
  128.4 0.7 copy.18
  129.1 3.1 %copy.19 = bf16[8,2,128,512]{3,2,1,0:T(8,128)(2,1)} copy(bf16[8,2,128,512]{3,2,1,0:T(8,128)(2,1)} %get-tuple-element.63) | data formatting | bytes 4194304
Async XLA Ops:
  0.6 37.5 %copy-start = (s32[4]{0:T(128)S(1)}, s32[4]{0:T(128)}, u32[]{:S(2)}) copy-start(s32[4]{0:T(128)} %length_ref.1) | copy-start | bytes 52
  0.6 37.5 %copy-start.1 = (s32[128]{0:T(128)S(1)}, s32[128]{0:T(128)}, u32[]{:S(2)}) copy-start(s32[128]{0:T(128)} %param.18) | copy-start | bytes 1540
